TPU v7x, 32 devices: a whole 2x2x4 slice. The times are simulated.
32 devices in a mesh: lat: 16 (over z, x, core), chan: 2 (over y).
Axes of the slice: x: 2, y: 2, z: 4, core: 2. Of those that a mesh axis runs over, the one named last changes fastest.
Arguments:
- spec_in: bfloat16 [384, 1, 256, 2, 384], P('lat', None, 'chan'), may hold values from -6 to 6
- legendre: float32 [384, 384, 384], P('lat'), may hold values from -0.4375 to 0.4375
- mode_slot: int32 [384], replicated, may hold values from 0 to 383, each once
- w_in: bfloat16 [512, 256], replicated, may hold values from -0.375 to 0.375
- b_in: float32 [512], replicated, may hold values from -3 to 3
- w_out: bfloat16 [256, 512], replicated, may hold values from -0.25 to 0.25
- kernel: float32 [256, 9], P('chan'), may hold values from -4 to 4
Outputs:
- spec_out: bfloat16 [384, 1, 256, 2, 384], P('lat', None, 'chan')
Inputs may be any that keep to these rules, and one draw needn't show every extreme that they name: mode_slot holds every number of 0 to 383 once.
All inputs are finite; a program needn't handle non-finite values.
Results may differ from a plain program's by a relative error of at most 0.0083.
Values may be sent and summed in bfloat16 or wider, within the bound.
A program may use at most 192 MiB of HBM per device.

v0:
```python
import functools
import math

import jax
import jax.numpy as jnp
from jax import lax
from jax.experimental import pallas as pl
from jax.experimental.pallas import tpu as pltpu
from jax.sharding import PartitionSpec as P

NLON = 768


def with_halo(array, sides, width):
    for axis, dim in sides:
        count, length = (lax.axis_size(axis), array.shape[dim])
        up = [(i, (i + 1) % count) for i in range(count - 1)]
        down = [(j, i) for i, j in up]
        last = lax.slice_in_dim(array, length - width, length, axis=dim)
        first = lax.slice_in_dim(array, 0, width, axis=dim)
        before = lax.ppermute(last, axis, up)
        after = lax.ppermute(first, axis, down)
        array = jnp.concatenate([before, array, after], axis=dim)
    return array


def wave_table(modes, count):
    columns = jnp.arange(count, dtype=jnp.int32)
    phase = modes[:, None] * columns[None, :] % count
    angle = phase.astype(jnp.float32) * (2.0 * math.pi / count)
    factor = count ** (-0.5)
    return jnp.stack([jnp.cos(angle) * factor, -jnp.sin(angle) * factor], axis=1)


def on_device(spec_in, legendre, mode_slot, w_in, b_in, w_out, kernel):
    high = lax.Precision.HIGHEST
    slots_here = legendre.shape[0]
    lat_index = lax.axis_index("lat")
    local_modes = lax.dynamic_slice_in_dim(mode_slot, lat_index * slots_here, slots_here)
    degrees = jnp.arange(legendre.shape[2], dtype=jnp.int32)
    masked = jnp.where(
        degrees[None, None, :] >= local_modes[:, None, None], legendre, jnp.float32(0.0)
    )
    waves = wave_table(mode_slot, NLON)
    coeff = jnp.einsum("sbcrl,stl->sbcrt", spec_in.astype(jnp.float32), masked, precision=high)
    grid = jnp.einsum(
        "sbcrt,srp->btcp",
        lax.all_to_all(coeff, "lat", split_axis=4, concat_axis=0, tiled=True),
        waves,
        precision=high,
    ).astype(jnp.bfloat16)
    batch, rows_here, chan_here, columns = grid.shape
    whole = lax.all_gather(grid, "chan", axis=2, tiled=True)
    chan_index = lax.axis_index("chan")
    w_local = lax.dynamic_slice_in_dim(w_out, chan_index * chan_here, chan_here, 0)
    pre = jnp.einsum("hc,btcp->bthp", w_in, whole, preferred_element_type=jnp.float32)
    hidden = jax.nn.gelu(pre + b_in[None, None, :, None], approximate=True).astype(jnp.bfloat16)
    branch = jnp.einsum("ch,bthp->btcp", w_local, hidden, preferred_element_type=jnp.float32)
    mixed = (grid.astype(jnp.float32) + branch).astype(jnp.bfloat16)
    half = columns // 2
    last_row = lax.axis_size("lat") - 1
    padded = with_halo(mixed, (("lat", 1),), 1)
    upper = jnp.where(lat_index == 0, jnp.roll(mixed[:, 0:1], half, axis=3), padded[:, 0:1])
    lower = jnp.where(lat_index == last_row, jnp.roll(mixed[:, -1:], half, axis=3), padded[:, -1:])
    stacked = jnp.concatenate([upper, padded[:, 1:-1], lower], axis=1).astype(jnp.float32)
    wide = mixed.astype(jnp.float32)
    conv = jnp.zeros_like(wide)
    for i in range(3):
        band = stacked[:, i : i + rows_here]
        for j in range(3):
            conv = conv + kernel[:, 3 * i + j][None, None, :, None] * jnp.roll(band, 1 - j, axis=3)
    field = wide + conv
    modes = jnp.einsum("btcp,srp->sbcrt", field, waves, precision=high)
    return jnp.einsum(
        "sbcrt,stl->sbcrl",
        lax.all_to_all(modes, "lat", split_axis=0, concat_axis=4, tiled=True),
        masked,
        precision=high,
    ).astype(jnp.bfloat16)


def all_taps(taps, axis):
    count, index, width = lax.axis_size(axis), lax.axis_index(axis), taps.shape[1]
    ring = [(i, (i + 1) % count) for i in range(count)]
    whole = jnp.zeros((taps.shape[0], count * width), taps.dtype)
    for step in range(count):
        owner = (index - step) % count
        whole = lax.dynamic_update_slice_in_dim(whole, taps, owner * width, 1)
        if step < count - 1:
            taps = lax.ppermute(taps, axis, ring)
    return whole


def conv_halo(mixed, axes):
    count, index = lax.axis_size(axes), lax.axis_index(axes)
    half = mixed.shape[1] // 2
    up = [(i, i + 1) for i in range(count - 1)]
    down = [(j, i) for i, j in up]
    before = lax.ppermute(mixed[-1], axes, up)
    after = lax.ppermute(mixed[0], axes, down)
    before = jnp.where(index == 0, jnp.roll(mixed[0], half, axis=0), before)
    after = jnp.where(index == count - 1, jnp.roll(mixed[-1], half, axis=0), after)
    return before, after


def grid_kernel(lats, chans, coeff_ref, waves_ref, w_in_ref, b_in_ref, w_out_ref, mixed_ref):
    rows, width = coeff_ref.shape[2], coeff_ref.shape[3]
    coeff = coeff_ref[...].reshape(lats, chans, rows, width)
    parts = [coeff[:, j].reshape(lats * rows, width) for j in range(chans)]
    merged = jnp.concatenate(parts, axis=1)
    grid = jnp.dot(waves_ref[...], merged, preferred_element_type=jnp.float32).astype(jnp.bfloat16)
    pre = jnp.dot(grid, w_in_ref[...], preferred_element_type=jnp.float32) + b_in_ref[...]
    hidden = jax.nn.gelu(pre, approximate=True).astype(jnp.bfloat16)
    branch = jnp.dot(hidden, w_out_ref[...], preferred_element_type=jnp.float32)
    mixed_ref[0] = (grid.astype(jnp.float32) + branch).astype(jnp.bfloat16)


def field_kernel(lats, chans, here_ref, prev_ref, next_ref, before_ref, after_ref, kernel_ref, waves_ref, modes_ref):
    row, last = pl.program_id(0), pl.num_programs(0) - 1
    here = here_ref[0].astype(jnp.float32)
    prev = jnp.where(row == 0, before_ref[...].astype(jnp.float32), prev_ref[0].astype(jnp.float32))
    after = jnp.where(row == last, after_ref[...].astype(jnp.float32), next_ref[0].astype(jnp.float32))
    count = here.shape[0]
    taps = [
        kernel_ref[j : j + 1] * prev + kernel_ref[3 + j : 4 + j] * here + kernel_ref[6 + j : 7 + j] * after
        for j in range(3)
    ]
    field = here + taps[1] + pltpu.roll(taps[0], 1, 0) + pltpu.roll(taps[2], count - 1, 0)
    modes = jnp.dot(waves_ref[...], field.astype(jnp.bfloat16), preferred_element_type=jnp.float32)
    modes = modes.astype(jnp.bfloat16)
    rows, width = modes_ref.shape[2], modes_ref.shape[3]
    for i in range(lats):
        for j in range(chans):
            modes_ref[i * chans + j, 0] = modes[i * rows : (i + 1) * rows, j * width : (j + 1) * width]


def on_device_rows(spec_in, legendre, mode_slot, w_in, b_in, w_out, kernel):
    axes = ("lat", "chan")
    lats, chans = lax.axis_size("lat"), lax.axis_size("chan")
    count = lats * chans
    slots, rows_all, degrees_all = legendre.shape
    width = spec_in.shape[2]
    rows = rows_all // count
    columns = NLON
    channels = width * chans
    lat_index = lax.axis_index("lat")
    local_modes = lax.dynamic_slice_in_dim(mode_slot, lat_index * slots, slots)
    degrees = jnp.arange(degrees_all, dtype=jnp.int32)
    keep = degrees[None, None, :] >= local_modes[:, None, None]
    masked = jnp.where(keep, legendre, jnp.float32(0.0)).astype(jnp.bfloat16)
    waves = wave_table(mode_slot, columns).astype(jnp.bfloat16)
    waves = jnp.swapaxes(waves.reshape(lats, slots, 2, columns), 1, 2).reshape(-1, columns)
    taps = all_taps(kernel.T, "chan")
    coeff = jnp.einsum("scrl,stl->trsc", spec_in[:, 0], masked, preferred_element_type=jnp.float32)
    coeff = coeff.astype(jnp.bfloat16).reshape(rows_all, 2 * slots, width)
    coeff = lax.all_to_all(coeff, axes, split_axis=0, concat_axis=0, tiled=True)
    coeff = coeff.reshape(count, rows, 2 * slots, width)
    packed = pl.BlockSpec((count, 1, 2 * slots, width), lambda t: (0, t, 0, 0))

    def whole(array):
        return pl.BlockSpec(array.shape, lambda t: (0,) * array.ndim)

    w_in_t, w_out_t, bias, waves_t = w_in.T, w_out.T, b_in[None, :], waves.T
    params = pltpu.CompilerParams(vmem_limit_bytes=48 * 1024 * 1024)

    def mixed_rows(steps, stride, name):
        work = columns * channels * (waves_t.shape[1] + 2 * w_in_t.shape[1])
        return pl.pallas_call(
            functools.partial(grid_kernel, lats, chans),
            grid=(steps,),
            out_shape=jax.ShapeDtypeStruct((steps, columns, channels), jnp.bfloat16),
            in_specs=[
                pl.BlockSpec((count, 1, 2 * slots, width), lambda t: (0, t * stride, 0, 0)),
                whole(waves_t), whole(w_in_t), whole(bias), whole(w_out_t),
            ],
            out_specs=pl.BlockSpec((1, columns, channels), lambda t: (t, 0, 0)),
            compiler_params=params,
            cost_estimate=pl.CostEstimate(
                flops=2 * steps * work, bytes_accessed=coeff.nbytes, transcendentals=0
            ),
            name=name,
        )(coeff, waves_t, w_in_t, bias, w_out_t)

    edges = mixed_rows(min(2, rows), max(rows - 1, 1), "grid_edges")
    before, after = conv_halo(edges, axes)
    mixed = mixed_rows(rows, 1, "grid_mlp")
    line = (1, columns, channels)
    modes = pl.pallas_call(
        functools.partial(field_kernel, lats, chans),
        grid=(rows,),
        out_shape=jax.ShapeDtypeStruct((count, rows, 2 * slots, width), jnp.bfloat16),
        in_specs=[
            pl.BlockSpec(line, lambda t: (t, 0, 0)),
            pl.BlockSpec(line, lambda t: (jnp.maximum(t - 1, 0), 0, 0)),
            pl.BlockSpec(line, lambda t: (jnp.minimum(t + 1, rows - 1), 0, 0)),
            whole(before),
            whole(after),
            whole(taps),
            whole(waves),
        ],
        out_specs=packed,
        compiler_params=params,
        name="conv_dft",
    )(mixed, mixed, mixed, before, after, taps, waves)
    modes = modes.reshape(rows_all, 2 * slots, width)
    modes = lax.all_to_all(modes, axes, split_axis=0, concat_axis=0, tiled=True)
    modes = modes.reshape(rows_all, 2, slots, width)
    out = jnp.einsum("trsc,stl->scrl", modes, masked, preferred_element_type=jnp.float32)
    return out.astype(jnp.bfloat16)[:, None]


def solution(mesh):
    in_specs = (
        P("lat", None, "chan", None, None),
        P("lat", None, None),
        P(),
        P(),
        P(),
        P(),
        P("chan", None),
    )
    out_specs = P("lat", None, "chan", None, None)
    count = mesh.shape["lat"] * mesh.shape["chan"]

    def call(spec_in, legendre, *rest):
        samples, rows_all = spec_in.shape[1], legendre.shape[1]
        by_rows = samples == 1 and rows_all % count == 0
        body = on_device_rows if by_rows else on_device
        return jax.shard_map(
            body, mesh=mesh, in_specs=in_specs, out_specs=out_specs, check_vma=False
        )(spec_in, legendre, *rest)

    return call
```

profile of v0, /device:TPU:11, one launch (start us, length us, event | category | flops | bytes accessed | tf_op | source)
XLA Modules:
  0.0 315.9 jit_solution(7115556850699575564)
XLA Ops:
  0.0 0.8 dynamic_slice.3
  0.8 0.1 iota_compare_fusion
  0.8 8.3 %convert_bitcast_fusion.1 = bf16[384,2,24,128]{3,0,1,2:T(8,128)(2,1)S(1)} fusion(bf16[24,128,2,384]{3,2,1,0:T(2,128)(2,1)} %bitcast.53, f32[24,384,384]{2,1,0:T(8,128)} %param.8, pred[24,384]{1,0:T(8,128)(4,1)S(1)} %iota_compare_fusion), kind=kOutput, calls=%fused_computation.7 | convolution fusion | flops 1817837568 | bytes 23602176 | tf_op jit(solution)/shard_map/scrl,stl->trsc/dot_general | solution.py:154
  9.2 5.2 %copy.16 = bf16[384,2,24,128]{3,2,1,0:T(8,128)(2,1)} copy(bf16[384,2,24,128]{3,0,1,2:T(8,128)(2,1)S(1)} %convert_bitcast_fusion.1) | data formatting | bytes 9437184 | tf_op jit(solution)/shard_map/convert_element_type | solution.py:155
  14.4 6.3 %all-to-all-start = ((bf16[384,48,128]{2,1,0:T(8,128)(2,1)}), bf16[384,48,128]{2,1,0:T(8,128)(2,1)}, u32[]{:S(2)}, u32[]{:S(2)}) async-start(bf16[384,48,128]{2,1,0:T(8,128)(2,1)} %bitcast.50), calls=%async_computation | async-start | bytes 9437184 | tf_op jit(solution)/shard_map/all_to_all | solution.py:156
  20.8 0.0 copy-start.1
  20.8 0.0 copy-start.2
  20.8 0.0 copy-start
  20.8 1.2 collective-permute-start.2
  22.1 0.1 mul.82
  22.2 5.4 %multiply_convert_fusion.1 = (bf16[16,24,1,768]{3,1,2,0:T(8,128)(2,1)S(1)}, bf16[16,24,1,768]{3,1,2,0:T(8,128)(2,1)S(1)}) fusion(s32[16,24]{1,0:T(8,128)S(1)} %mul.82), kind=kLoop, calls=%fused_computation.13 | loop fusion | flops 4128768 | bytes 1181184 | tf_op jit(solution)/shard_map/convert | solution.py:229
  27.6 0.1 pad_maximum_fusion
  27.8 0.6 copy.19.waves_ref
  28.4 0.0 copy-done.1
  28.4 0.1 copy.17
  28.6 0.1 copy.18
  28.7 17.5 %collective-permute-done.2 = f32[9,128]{1,0:T(8,128)S(1)} collective-permute-done((f32[9,128]{1,0:T(8,128)S(1)}, f32[9,128]{1,0:T(8,128)S(1)}, u32[]{:S(2)}, u32[]{:S(2)}) %collective-permute-start.2) | collective-permute-done | bytes 4640 | tf_op jit(solution)/shard_map/ppermute | solution.py:90
  46.2 76.4 %all-to-all-done = bf16[384,48,128]{2,1,0:T(8,128)(2,1)} async-done(((bf16[384,48,128]{2,1,0:T(8,128)(2,1)}), bf16[384,48,128]{2,1,0:T(8,128)(2,1)}, u32[]{:S(2)}, u32[]{:S(2)}) %all-to-all-start) | async-done | bytes 4718624 | tf_op jit(solution)/shard_map/all_to_all | solution.py:156
  122.6 4.2 %grid_edges.1 = bf16[2,768,256]{2,1,0:T(8,128)(2,1)S(1)} custom-call(bf16[32,12,48,128]{3,2,1,0:T(8,128)(2,1)} %bitcast.6.coeff_ref, bf16[768,768]{1,0:T(8,128)(2,1)S(1)} %copy.19.waves_ref, bf16[256,512]{1,0:T(8,128)(2,1)S(1)} %bitcast.44, f32[1,512]{1,0:T(1,128)S(1)} %bitcast.48, bf16[512,256]{1,0:T(8,128)(2,1)S(1)} %bitcast.46), custom_call_target="tpu_custom_call" | custom-call | flops 1409286144 | bytes 4718592 | tf_op jit(solution)/shard_map/grid_edges/pallas_call | solution.py:168
  126.9 0.1 slice_bitcast_fusion
  126.9 3.5 %collective-permute-start = (bf16[768,256]{1,0:T(8,128)(2,1)S(1)}, bf16[768,256]{1,0:T(8,128)(2,1)S(1)}, u32[]{:S(2)}, u32[]{:S(2)}) collective-permute-start(bf16[768,256]{1,0:T(8,128)(2,1)S(1)} %get-tuple-element.10), channel_id=1, source_target_pairs={{0,1},{1,2},{2,3},{3,4},{4,5},{5,6},{6,7},{7,8},{8,9},{9,10},{10,1... | collective-permute-start | bytes 1179656 | tf_op jit(solution)/shard_map/ppermute | solution.py:99
  130.5 21.1 %grid_mlp.1.here_ref.prev_ref.next_ref = bf16[12,768,256]{2,1,0:T(8,128)(2,1)} custom-call(bf16[32,12,48,128]{3,2,1,0:T(8,128)(2,1)} %bitcast.6.coeff_ref, bf16[768,768]{1,0:T(8,128)(2,1)S(1)} %copy.19.waves_ref, bf16[256,512]{1,0:T(8,128)(2,1)S(1)} %bitcast.45, f32[1,512]{1,0:T(1,128)S(1)} %bitcast.49, bf16[512,256]{1,0:T(8,128)(2,1)S(1)} %bitcast.47), custom_call_target="tpu_custom_call" | custom-call | flops 8455716864 | bytes 4718592 | tf_op jit(solution)/shard_map/grid_mlp/pallas_call | solution.py:168
  151.6 2.2 collective-permute-start.1
  153.8 0.1 slice_bitcast_fusion.3
  153.9 0.0 collective-permute-done
  153.9 0.1 maximum_select_fusion.before_ref
  154.0 10.0 %collective-permute-done.1 = bf16[768,256]{1,0:T(8,128)(2,1)S(1)} collective-permute-done((bf16[768,256]{1,0:T(8,128)(2,1)S(1)}, bf16[768,256]{1,0:T(8,128)(2,1)S(1)}, u32[]{:S(2)}, u32[]{:S(2)}) %collective-permute-start.1) | collective-permute-done | bytes 393248 | tf_op jit(solution)/shard_map/ppermute | solution.py:100
  164.0 0.1 maximum_select_fusion.1.after_ref
  164.1 17.3 %conv_dft.1 = bf16[32,12,48,128]{3,2,1,0:T(8,128)(2,1)} custom-call(bf16[12,768,256]{2,1,0:T(8,128)(2,1)} %grid_mlp.1.here_ref.prev_ref.next_ref, bf16[12,768,256]{2,1,0:T(8,128)(2,1)} %grid_mlp.1.here_ref.prev_ref.next_ref, bf16[12,768,256]{2,1,0:T(8,128)(2,1)} %grid_mlp.1.here_ref.prev_ref.next_ref, bf16[768,256]{1,0:T(8,128)(2,1)S(1)} %maximum_select_fusion.before_ref, ...), custom_call_target="tpu_custom_call" | custom-call | tf_op jit(solution)/shard_map/conv_dft/pallas_call | solution.py:188
  181.4 110.1 %all_to_all.10 = bf16[384,48,128]{2,1,0:T(8,128)(2,1)} all-to-all(bf16[384,48,128]{2,1,0:T(8,128)(2,1)} %bitcast.51), channel_id=1, replica_groups=mesh['lat'=16,'chan'=2] {'lat','chan'}, dimensions={0} | all-to-all | bytes 9437184 | tf_op jit(solution)/shard_map/all_to_all | solution.py:206
  291.6 12.0 %convert_bitcast_fusion = bf16[24,1,128,2,384]{2,4,3,0,1:T(8,128)(2,1)} fusion(bf16[384,2,24,128]{3,2,1,0:T(8,128)(2,1)} %bitcast.52, f32[24,384,384]{2,1,0:T(8,128)} %param.8, pred[24,384]{1,0:T(8,128)(4,1)S(1)} %iota_compare_fusion), kind=kOutput, calls=%fused_computation.6 | convolution fusion | flops 1817837568 | bytes 23602176 | tf_op jit(solution)/shard_map/trsc,stl->scrl/dot_general | solution.py:208
  303.6 12.4 %copy.23 = bf16[24,1,128,2,384]{4,3,2,1,0:T(2,128)(2,1)} copy(bf16[24,1,128,2,384]{2,4,3,0,1:T(8,128)(2,1)} %convert_bitcast_fusion) | data formatting | bytes 9437184 | tf_op jit(solution)/shard_map/broadcast_in_dim | solution.py:209
  (9 shorter events, 0.0 us)
Async XLA Ops:
  14.4 6.4 %copy-start.3 = (f32[128,9]{0,1:T(8,128)S(1)}, f32[128,9]{0,1:T(8,128)}, u32[]{:S(2)}) copy-start(f32[128,9]{0,1:T(8,128)} %param.13) | copy-start | bytes 13828
  14.4 7.7 %copy-start.4 = (s32[384]{0:T(512)S(1)}, s32[384]{0:T(512)}, u32[]{:S(2)}) copy-start(s32[384]{0:T(512)} %param.9) | copy-start | bytes 4612
  14.4 108.2 %all-to-all-start = ((bf16[384,48,128]{2,1,0:T(8,128)(2,1)}), bf16[384,48,128]{2,1,0:T(8,128)(2,1)}, u32[]{:S(2)}, u32[]{:S(2)}) async-start(bf16[384,48,128]{2,1,0:T(8,128)(2,1)} %bitcast.50), calls=%async_computation | async-start | bytes 9437184 | tf_op jit(solution)/shard_map/all_to_all | solution.py:156
  20.8 7.7 %copy-start.1 = (bf16[512,256]{1,0:T(8,128)(2,1)S(1)}, bf16[512,256]{1,0:T(8,128)(2,1)}, u32[]{:S(2)}) copy-start(bf16[512,256]{1,0:T(8,128)(2,1)} %param.10) | copy-start | bytes 786436
  20.8 7.8 %copy-start.2 = (bf16[256,512]{1,0:T(8,128)(2,1)S(1)}, bf16[256,512]{1,0:T(8,128)(2,1)}, u32[]{:S(2)}) copy-start(bf16[256,512]{1,0:T(8,128)(2,1)} %param.12) | copy-start | bytes 786436
  20.8 101.9 %copy-start = (f32[512]{0:T(512)S(1)}, f32[512]{0:T(512)}, u32[]{:S(2)}) copy-start(f32[512]{0:T(512)} %param.11) | copy-start | bytes 6148
  20.8 25.4 %collective-permute-start.2 = (f32[9,128]{1,0:T(8,128)S(1)}, f32[9,128]{1,0:T(8,128)S(1)}, u32[]{:S(2)}, u32[]{:S(2)}) collective-permute-start(f32[9,128]{1,0:T(8,128)S(1)} %bitcast.54), channel_id=1, source_target_pairs={{0,1},{1,0},{2,3},{3,2},{4,5},{5,4},{6,7},{7,6},{8,9},{9,8},{10,11... | collective-permute-start | bytes 13832 | tf_op jit(solution)/shard_map/ppermute | solution.py:90
  126.9 26.9 %collective-permute-start = (bf16[768,256]{1,0:T(8,128)(2,1)S(1)}, bf16[768,256]{1,0:T(8,128)(2,1)S(1)}, u32[]{:S(2)}, u32[]{:S(2)}) collective-permute-start(bf16[768,256]{1,0:T(8,128)(2,1)S(1)} %get-tuple-element.10), channel_id=1, source_target_pairs={{0,1},{1,2},{2,3},{3,4},{4,5},{5,6},{6,7},{7,8},{8,9},{9,10},{10,1... | collective-permute-start | bytes 1179656 | tf_op jit(solution)/shard_map/ppermute | solution.py:99
  151.6 12.4 %collective-permute-start.1 = (bf16[768,256]{1,0:T(8,128)(2,1)S(1)}, bf16[768,256]{1,0:T(8,128)(2,1)S(1)}, u32[]{:S(2)}, u32[]{:S(2)}) collective-permute-start(bf16[768,256]{1,0:T(8,128)(2,1)S(1)} %get-tuple-element.9), channel_id=1, source_target_pairs={{1,0},{2,1},{3,2},{4,3},{5,4},{6,5},{7,6},{8,7},{9,8},{10,9},{11,1... | collective-permute-start | bytes 1179656 | tf_op jit(solution)/shard_map/ppermute | solution.py:100
where the time goes:
time: 320 us; the launch traced here: 316 us
  blocking collectives  110 us (34%)
  waiting for transfers between devices  104 us (32%)
  Pallas kernels  42.6 us (13%)
  matrix products  20.3 us (6%)
  local copies, waits for them, and re-layouts  19.5 us (6%)
  starting transfers between devices  13.4 us (4%)
  other arithmetic  5.81 us (2%)
    all_to_all x1, blocking collectives, on_device_rows(): modes = lax.all_to_all(modes, axes, split_axis=0, concat_axis=0, tiled=True)  110 us
    all_to_all x1, waiting for transfers between devices, on_device_rows(): coeff = lax.all_to_all(coeff, axes, split_axis=0, concat_axis=0, tiled=True)  76.4 us
    pallas_call x2, Pallas kernels, mixed_rows(): pl.pallas_call(functools.partial(grid_kernel, lats, chans), grid=(steps,)...  25.3 us
    ppermute x1, waiting for transfers between devices, all_taps(): taps = lax.ppermute(taps, axis, ring)  17.5 us
    pallas_call x1, Pallas kernels, on_device_rows(): pl.pallas_call(functools.partial(field_kernel, lats, chans), grid=(rows,)...  17.3 us
    broadcast_in_dim x1, local copies, waits for them, and re-layouts, on_device_rows(): return out.astype(jnp.bfloat16)[:, None]  12.4 us
    dot_general x1, matrix products, on_device_rows(): jnp.einsum('trsc,stl->scrl', modes, masked, preferred_element_type=jnp.fl...  12 us
    ppermute x1, waiting for transfers between devices, conv_halo(): after = lax.ppermute(mixed[0], axes, down)  10 us
  transfers between devices with their start and end apart: 4, of which 3 were waited for; matrix products, arithmetic and copies ran while one was open for 2% of the time, Pallas kernels for 7%

commit v1 on v0

v1 whole, which is shorter than its diff:
```python
import functools
import math

import jax
import jax.numpy as jnp
from jax import lax
from jax.experimental import pallas as pl
from jax.experimental.pallas import tpu as pltpu
from jax.sharding import PartitionSpec as P

NLON = 768


def with_halo(array, sides, width):
    for axis, dim in sides:
        count, length = (lax.axis_size(axis), array.shape[dim])
        up = [(i, (i + 1) % count) for i in range(count - 1)]
        down = [(j, i) for i, j in up]
        last = lax.slice_in_dim(array, length - width, length, axis=dim)
        first = lax.slice_in_dim(array, 0, width, axis=dim)
        before = lax.ppermute(last, axis, up)
        after = lax.ppermute(first, axis, down)
        array = jnp.concatenate([before, array, after], axis=dim)
    return array


def wave_table(modes, count):
    columns = jnp.arange(count, dtype=jnp.int32)
    phase = modes[:, None] * columns[None, :] % count
    angle = phase.astype(jnp.float32) * (2.0 * math.pi / count)
    factor = count ** (-0.5)
    return jnp.stack([jnp.cos(angle) * factor, -jnp.sin(angle) * factor], axis=1)


def on_device(spec_in, legendre, mode_slot, w_in, b_in, w_out, kernel):
    high = lax.Precision.HIGHEST
    slots_here = legendre.shape[0]
    lat_index = lax.axis_index("lat")
    local_modes = lax.dynamic_slice_in_dim(mode_slot, lat_index * slots_here, slots_here)
    degrees = jnp.arange(legendre.shape[2], dtype=jnp.int32)
    masked = jnp.where(
        degrees[None, None, :] >= local_modes[:, None, None], legendre, jnp.float32(0.0)
    )
    waves = wave_table(mode_slot, NLON)
    coeff = jnp.einsum("sbcrl,stl->sbcrt", spec_in.astype(jnp.float32), masked, precision=high)
    grid = jnp.einsum(
        "sbcrt,srp->btcp",
        lax.all_to_all(coeff, "lat", split_axis=4, concat_axis=0, tiled=True),
        waves,
        precision=high,
    ).astype(jnp.bfloat16)
    batch, rows_here, chan_here, columns = grid.shape
    whole = lax.all_gather(grid, "chan", axis=2, tiled=True)
    chan_index = lax.axis_index("chan")
    w_local = lax.dynamic_slice_in_dim(w_out, chan_index * chan_here, chan_here, 0)
    pre = jnp.einsum("hc,btcp->bthp", w_in, whole, preferred_element_type=jnp.float32)
    hidden = jax.nn.gelu(pre + b_in[None, None, :, None], approximate=True).astype(jnp.bfloat16)
    branch = jnp.einsum("ch,bthp->btcp", w_local, hidden, preferred_element_type=jnp.float32)
    mixed = (grid.astype(jnp.float32) + branch).astype(jnp.bfloat16)
    half = columns // 2
    last_row = lax.axis_size("lat") - 1
    padded = with_halo(mixed, (("lat", 1),), 1)
    upper = jnp.where(lat_index == 0, jnp.roll(mixed[:, 0:1], half, axis=3), padded[:, 0:1])
    lower = jnp.where(lat_index == last_row, jnp.roll(mixed[:, -1:], half, axis=3), padded[:, -1:])
    stacked = jnp.concatenate([upper, padded[:, 1:-1], lower], axis=1).astype(jnp.float32)
    wide = mixed.astype(jnp.float32)
    conv = jnp.zeros_like(wide)
    for i in range(3):
        band = stacked[:, i : i + rows_here]
        for j in range(3):
            conv = conv + kernel[:, 3 * i + j][None, None, :, None] * jnp.roll(band, 1 - j, axis=3)
    field = wide + conv
    modes = jnp.einsum("btcp,srp->sbcrt", field, waves, precision=high)
    return jnp.einsum(
        "sbcrt,stl->sbcrl",
        lax.all_to_all(modes, "lat", split_axis=0, concat_axis=4, tiled=True),
        masked,
        precision=high,
    ).astype(jnp.bfloat16)


def rows_kernel(lats, chans, coeff_ref, waves_t_ref, waves_ref, w_in_ref, b_in_ref, w_out_ref, modes_ref,
                recv, send, fwd_sent, fwd_got, bwd_sent, bwd_got):
    chunks, count, rows, depth, width = coeff_ref.shape
    lat, chan = lax.axis_index("lat"), lax.axis_index("chan")
    me = lat * chans + chan

    def landing(k):
        return recv.at[k, :, chan, pl.ds(lat * depth, depth), :]

    def leaving(k, to):
        return send.at[k, :, to % chans, pl.ds((to // chans) * depth, depth), :]

    def forward(k, _):
        def to_peer(i, _):
            to = (me + i) % count
            pltpu.make_async_remote_copy(
                src_ref=coeff_ref.at[k, to], dst_ref=landing(k),
                send_sem=fwd_sent, recv_sem=fwd_got.at[k],
                device_id=(to // chans, to % chans), device_id_type=pl.DeviceIdType.MESH,
            ).start()
            return 0

        pltpu.make_async_copy(coeff_ref.at[k, me], landing(k), fwd_got.at[k]).start()
        return lax.fori_loop(1, count, to_peer, 0)

    lax.fori_loop(0, chunks, forward, 0)

    def one_chunk(k, _):
        pltpu.make_async_copy(recv.at[k], recv.at[k], fwd_got.at[k]).wait()

        def one_row(j, _):
            merged = jnp.concatenate([recv[k, j, i] for i in range(chans)], axis=1)
            grid = jnp.dot(waves_t_ref[...], merged, preferred_element_type=jnp.float32).astype(jnp.bfloat16)
            pre = jnp.dot(grid, w_in_ref[...], preferred_element_type=jnp.float32) + b_in_ref[...]
            hidden = jax.nn.gelu(pre, approximate=True).astype(jnp.bfloat16)
            branch = jnp.dot(hidden, w_out_ref[...], preferred_element_type=jnp.float32)
            mixed = (grid.astype(jnp.float32) + branch).astype(jnp.bfloat16)
            modes = jnp.dot(waves_ref[...], mixed, preferred_element_type=jnp.float32).astype(jnp.bfloat16)
            for i in range(chans):
                send[k, j, i] = modes[:, i * width : (i + 1) * width]
            return 0

        lax.fori_loop(0, rows, one_row, 0)

        def to_peer(i, _):
            to = (me + i) % count
            pltpu.make_async_remote_copy(
                src_ref=leaving(k, to), dst_ref=modes_ref.at[k, me],
                send_sem=bwd_sent, recv_sem=bwd_got,
                device_id=(to // chans, to % chans), device_id_type=pl.DeviceIdType.MESH,
            ).start()
            return 0

        pltpu.make_async_copy(leaving(k, me), modes_ref.at[k, me], bwd_got).start()
        return lax.fori_loop(1, count, to_peer, 0)

    lax.fori_loop(0, chunks, one_chunk, 0)
    away = coeff_ref.at[:, pl.ds(0, count - 1)]
    pltpu.make_async_copy(away, away, fwd_sent).wait()
    away = modes_ref.at[:, pl.ds(0, count - 1)]
    pltpu.make_async_copy(away, away, bwd_sent).wait()
    pltpu.make_async_copy(modes_ref, modes_ref, bwd_got).wait()


def spectral_filters(kernel, modes, count):
    angle = modes.astype(jnp.float32) * (2.0 * math.pi / count)
    cosine, sine = jnp.cos(angle)[:, None], jnp.sin(angle)[:, None]
    pairs = []
    for i in range(3):
        left, here, right = (kernel[:, 3 * i + j][None, :] for j in range(3))
        pairs.append((here + (left + right) * cosine + (1.0 if i == 1 else 0.0), (right - left) * sine))
    return pairs


def on_device_rows(spec_in, legendre, mode_slot, w_in, b_in, w_out, kernel):
    lats, chans = lax.axis_size("lat"), lax.axis_size("chan")
    count = lats * chans
    slots, rows_all, degrees_all = legendre.shape
    width = spec_in.shape[2]
    own_rows = rows_all // count
    chunks = next(k for k in (4, 3, 2, 1) if own_rows % k == 0)
    rows = own_rows // chunks
    columns = NLON
    lat_index = lax.axis_index("lat")
    local_modes = lax.dynamic_slice_in_dim(mode_slot, lat_index * slots, slots)
    degrees = jnp.arange(degrees_all, dtype=jnp.int32)
    keep = degrees[None, None, :] >= local_modes[:, None, None]
    masked = jnp.where(keep, legendre, jnp.float32(0.0)).astype(jnp.bfloat16)
    waves = wave_table(mode_slot, columns).astype(jnp.bfloat16)
    waves = jnp.swapaxes(waves.reshape(lats, slots, 2, columns), 1, 2).reshape(-1, columns)
    coeff = jnp.einsum("scrl,stl->trsc", spec_in[:, 0], masked, preferred_element_type=jnp.float32)
    coeff = coeff.astype(jnp.bfloat16).reshape(chunks, count, rows, 2 * slots, width)
    hbm, vmem = pl.BlockSpec(memory_space=pl.ANY), pl.BlockSpec(memory_space=pltpu.VMEM)
    modes = pl.pallas_call(
        functools.partial(rows_kernel, lats, chans),
        out_shape=jax.ShapeDtypeStruct(coeff.shape, jnp.bfloat16),
        in_specs=[hbm] + [vmem] * 5,
        out_specs=hbm,
        scratch_shapes=[
            pltpu.VMEM((chunks, rows, chans, lats * 2 * slots, width), jnp.bfloat16),
            pltpu.VMEM((chunks, rows, chans, lats * 2 * slots, width), jnp.bfloat16),
            pltpu.SemaphoreType.DMA,
            pltpu.SemaphoreType.DMA((chunks,)),
            pltpu.SemaphoreType.DMA,
            pltpu.SemaphoreType.DMA,
        ],
        compiler_params=pltpu.CompilerParams(vmem_limit_bytes=48 * 1024 * 1024, has_side_effects=True),
        name="rows",
    )(coeff, waves.T, waves, w_in.T, b_in[None, :], w_out.T)
    modes = modes.reshape(rows_all, 2, slots, width).astype(jnp.float32)
    sign = jnp.where(local_modes % 2 == 0, 1.0, -1.0)[None, None, :, None]
    above = jnp.concatenate([modes[:1] * sign, modes[:-1]], axis=0)
    below = jnp.concatenate([modes[1:], modes[-1:] * sign], axis=0)
    real = imag = 0.0
    for (a, b), x in zip(spectral_filters(kernel, local_modes, columns), (above, modes, below)):
        real = real + a * x[:, 0] - b * x[:, 1]
        imag = imag + a * x[:, 1] + b * x[:, 0]
    field = jnp.stack([real, imag], axis=1).astype(jnp.bfloat16)
    out = jnp.einsum("trsc,stl->scrl", field, masked, preferred_element_type=jnp.float32)
    return out.astype(jnp.bfloat16)[:, None]


def solution(mesh):
    in_specs = (
        P("lat", None, "chan", None, None),
        P("lat", None, None),
        P(),
        P(),
        P(),
        P(),
        P("chan", None),
    )
    out_specs = P("lat", None, "chan", None, None)
    count = mesh.shape["lat"] * mesh.shape["chan"]

    def call(spec_in, legendre, *rest):
        samples, rows_all = spec_in.shape[1], legendre.shape[1]
        by_rows = samples == 1 and rows_all % count == 0
        body = on_device_rows if by_rows else on_device
        return jax.shard_map(
            body, mesh=mesh, in_specs=in_specs, out_specs=out_specs, check_vma=False
        )(spec_in, legendre, *rest)

    return call
```

time: 320 us -> 302 us (0.944); the launches traced: 316 us -> 301 us
  Pallas kernels: 42.6 us -> 212 us
  blocking collectives: 110 us -> 0 us
  waiting for transfers between devices: 104 us -> 0 us
  local copies, waits for them, and re-layouts: 19.5 us -> 53.7 us
  starting transfers between devices: 13.4 us -> 0 us
  other arithmetic: 5.81 us -> 18.9 us
  matrix products: 20.3 us -> 16.3 us
    pallas_call x3 -> x1, Pallas kernels: 42.6 us -> 212 us  [on_device_rows(): pl.pallas_call(functools.partial(rows_kernel, lats, chans), out_shape=jax...]
    all_to_all x1 -> x0, blocking collectives: 110 us -> none  [on_device_rows(): modes = lax.all_to_all(modes, axes, split_axis=0, concat_axis=0, tiled=True)]
    all_to_all x1 -> x0, waiting for transfers between devices: 76.4 us -> none  [on_device_rows(): coeff = lax.all_to_all(coeff, axes, split_axis=0, concat_axis=0, tiled=True)]
    ppermute x3 -> x0, waiting for transfers between devices: 27.5 us -> none  [the longest x1 17.5 us: all_taps(): taps = lax.ppermute(taps, axis, ring)]
    unnamed x12 -> x20, local copies, waits for them, and re-layouts: 0.3 us -> 19.9 us
    slice x1 -> x3, local copies, waits for them, and re-layouts: 0.05 us -> 15.5 us  [the longest x2 12.4 us: on_device_rows(): below = jnp.concatenate([modes[1:], modes[-1:] * sign], axis=0)]
    another operation x1 -> x3, other arithmetic: 5.43 us -> 16.8 us  [call(): jax.shard_map(body, mesh=mesh, in_specs=in_specs, out_specs=out_specs, ch...]
    ppermute x3 -> x0, starting transfers between devices: 7.01 us -> none  [the longest x1 3.52 us: conv_halo(): before = lax.ppermute(mixed[-1], axes, up)]
  transfers between devices with their start and end apart: 4 -> 0, of which waited for: 3 -> 0; matrix products, arithmetic and copies ran while one was open for 2% -> 0% of each run, Pallas kernels for 7% -> 0%
where the time goes in v1:
time: 302 us; the launch traced here: 301 us
  Pallas kernels  212 us (70%)
  local copies, waits for them, and re-layouts  53.7 us (18%)
  other arithmetic  18.9 us (6%)
  matrix products  16.3 us (5%)
    pallas_call x1, Pallas kernels, on_device_rows(): pl.pallas_call(functools.partial(rows_kernel, lats, chans), out_shape=jax...  212 us
    unnamed x20, local copies, waits for them, and re-layouts  19.9 us
    another operation x3, other arithmetic, call(): jax.shard_map(body, mesh=mesh, in_specs=in_specs, out_specs=out_specs, ch...  16.8 us
    slice x2, local copies, waits for them, and re-layouts, on_device_rows(): below = jnp.concatenate([modes[1:], modes[-1:] * sign], axis=0)  12.4 us
    broadcast_in_dim x1, local copies, waits for them, and re-layouts, on_device_rows(): return out.astype(jnp.bfloat16)[:, None]  12.4 us
    dot_general x1, matrix products, on_device_rows(): jnp.einsum('scrl,stl->trsc', spec_in[:, 0], masked, preferred_element_typ...  8.33 us
    dot_general x1, matrix products, on_device_rows(): jnp.einsum('trsc,stl->scrl', field, masked, preferred_element_type=jnp.fl...  8.02 us

profile of v1, /device:TPU:11, one launch (start us, length us, event | category | flops | bytes accessed | tf_op | source)
XLA Modules:
  0.0 301.3 jit_solution(5752450545194196220)
XLA Ops:
  0.0 0.8 compare_select_fusion.2
  0.8 1.0 slice_bitcast_fusion.2
  1.8 0.1 multiply_add_fusion.1
  1.9 0.1 iota_compare_fusion
  2.0 8.3 %convert_bitcast_fusion.1 = bf16[384,2,24,128]{3,0,1,2:T(8,128)(2,1)S(1)} fusion(bf16[24,128,2,384]{3,2,1,0:T(2,128)(2,1)} %bitcast.56, f32[24,384,384]{2,1,0:T(8,128)} %param.8, pred[24,384]{1,0:T(8,128)(4,1)S(1)} %iota_compare_fusion), kind=kOutput, calls=%fused_computation.19 | convolution fusion | flops 1817837568 | bytes 23602176 | tf_op jit(solution)/shard_map/scrl,stl->trsc/dot_general | solution.py:172
  10.3 0.0 copy-start.5
  10.3 5.2 %copy.9 = bf16[384,2,24,128]{3,2,1,0:T(8,128)(2,1)} copy(bf16[384,2,24,128]{3,0,1,2:T(8,128)(2,1)S(1)} %convert_bitcast_fusion.1) | data formatting | bytes 9437184 | tf_op jit(solution)/shard_map/convert_element_type | solution.py:173
  15.5 0.0 copy-done.5
  15.5 0.1 mul.285
  15.6 5.4 %multiply_convert_fusion.1 = (bf16[16,24,1,768]{3,1,2,0:T(8,128)(2,1)S(1)}, bf16[16,24,1,768]{3,1,2,0:T(8,128)(2,1)S(1)}) fusion(s32[16,24]{1,0:T(8,128)S(1)} %mul.285), kind=kLoop, calls=%fused_computation.25 | loop fusion | flops 4128768 | bytes 1181184 | tf_op jit(solution)/shard_map/convert.3 | solution.py:221
  21.1 0.1 pad_maximum_fusion.2
  21.2 0.6 copy.12.waves_t_ref
  21.8 0.0 copy-done.3
  21.8 0.1 copy.10
  22.0 0.0 copy-done.4
  22.0 0.1 copy.11
  22.1 0.0 copy-done
  22.2 212.2 %rows.1 = bf16[4,32,3,48,128]{4,3,2,1,0:T(8,128)(2,1)} custom-call(bf16[4,32,3,48,128]{4,3,2,1,0:T(8,128)(2,1)} %bitcast.55, bf16[768,768]{1,0:T(8,128)(2,1)S(1)} %copy.12.waves_t_ref, bf16[768,768]{1,0:T(8,128)(2,1)S(1)} %bitcast.46, bf16[256,512]{1,0:T(8,128)(2,1)S(1)} %bitcast.47, f32[1,512]{1,0:T(1,128)S(1)} %bitcast.49, bf16[512,256]{1,0:T(8,128)(2,1)S(1)} %bitcast.48), custom_call_target="tpu_custom_call" | custom-call | tf_op jit(solution)/shard_map/rows/pallas_call | solution.py:175
  234.4 0.7 fusion.27
  235.1 0.1 copy_multiply_fusion
  235.2 11.7 %fusion.26 = (f32[383,2,24,128]{3,2,1,0:T(8,128)}, f32[383,2,24,128]{3,2,1,0:T(8,128)}) fusion(bf16[384,2,24,128]{3,2,1,0:T(8,128)(2,1)} %bitcast.51), kind=kLoop, calls=%fused_computation.59 | loop fusion | bytes 37650432 | tf_op jit(solution)/shard_map/slice | solution.py:194
  246.9 6.7 %copy.26 = f32[383,2,24,128]{3,0,1,2:T(8,128)S(1)} copy(f32[383,2,24,128]{3,2,1,0:T(8,128)} %get-tuple-element.8) | data formatting | bytes 18825216
  253.6 0.0 slice-start
  253.6 0.0 slice-start.1
  253.6 10.5 %copy.29 = f32[383,2,24,128]{3,0,1,2:T(8,128)} copy(f32[383,2,24,128]{3,2,1,0:T(8,128)} %get-tuple-element.7) | data formatting | bytes 18825216
  264.2 0.0 slice-done
  264.2 3.0 fusion.28
  267.2 2.4 copy-done.1
  269.6 6.1 %subtract_convert_fusion = bf16[384,1,24,128]{3,0,1,2:T(8,128)(2,1)S(1)} fusion(f32[384,1,24,128]{3,2,1,0:T(8,128)} %get-tuple-element.12, f32[384,1,24,128]{3,2,1,0:T(8,128)S(1)} %get-tuple-element.11, f32[24,128]{1,0:T(8,128)S(1)} %get-tuple-element.34, f32[24,128]{1,0:T(8,128)S(1)} %get-tuple-element.28, f32[24,128]{1,0:T(8,128)S(1)} %get-tuple-element.35, ...), kind=kLoop, calls=%fused_computation.18 | loop fusion | flops 18874368 | bytes 30744576 | tf_op jit(solution)/shard_map/convert.1 | solution.py:221
  275.7 5.3 %add_convert_fusion = bf16[384,1,24,128]{3,0,1,2:T(8,128)(2,1)S(1)} fusion(f32[384,1,24,128]{3,2,1,0:T(8,128)S(1)} %copy-done.2, f32[384,1,24,128]{3,2,1,0:T(8,128)S(1)} %get-tuple-element.11, f32[24,128]{1,0:T(8,128)S(1)} %get-tuple-element.34, f32[24,128]{1,0:T(8,128)S(1)} %get-tuple-element.28, f32[24,128]{1,0:T(8,128)S(1)} %get-tuple-element.35, ...), kind=kLoop, calls=%fused_computation.17 | loop fusion | flops 18874368 | bytes 30744576 | tf_op jit(solution)/shard_map/convert.2 | solution.py:221
  280.9 8.0 %convert_bitcast_fusion = bf16[24,1,128,2,384]{2,4,3,0,1:T(8,128)(2,1)} fusion(bf16[384,1,24,128]{3,0,1,2:T(8,128)(2,1)S(1)} %add_convert_fusion, bf16[384,1,24,128]{3,0,1,2:T(8,128)(2,1)S(1)} %subtract_convert_fusion, f32[24,384,384]{2,1,0:T(8,128)} %param.8, pred[24,384]{1,0:T(8,128)(4,1)S(1)} %iota_compare_fusion), kind=kOutput, calls=%fused_computation.16 | convolution fusion | flops 1827274752 | bytes 23602176 | tf_op jit(solution)/shard_map/trsc,stl->scrl/dot_general | solution.py:200
  288.9 12.4 %copy.20 = bf16[24,1,128,2,384]{4,3,2,1,0:T(2,128)(2,1)} copy(bf16[24,1,128,2,384]{2,4,3,0,1:T(8,128)(2,1)} %convert_bitcast_fusion) | data formatting | bytes 9437184 | tf_op jit(solution)/shard_map/broadcast_in_dim | solution.py:201
  (9 shorter events, 0.1 us)
Async XLA Ops:
  10.3 5.2 %copy-start.5 = (s32[384]{0:T(512)S(1)}, s32[384]{0:T(512)}, u32[]{:S(2)}) copy-start(s32[384]{0:T(512)} %param.9) | copy-start | bytes 4612
  15.5 6.3 %copy-start.3 = (bf16[512,256]{1,0:T(8,128)(2,1)S(1)}, bf16[512,256]{1,0:T(8,128)(2,1)}, u32[]{:S(2)}) copy-start(bf16[512,256]{1,0:T(8,128)(2,1)} %param.10) | copy-start | bytes 786436
  15.5 6.5 %copy-start.4 = (bf16[256,512]{1,0:T(8,128)(2,1)S(1)}, bf16[256,512]{1,0:T(8,128)(2,1)}, u32[]{:S(2)}) copy-start(bf16[256,512]{1,0:T(8,128)(2,1)} %param.12) | copy-start | bytes 786436
  15.5 6.6 %copy-start = (f32[512]{0:T(512)S(1)}, f32[512]{0:T(512)}, u32[]{:S(2)}) copy-start(f32[512]{0:T(512)} %param.11) | copy-start | bytes 6148
  253.6 10.5 %slice-start = ((s8[4718592]{0:T(1024)(128)(4,1)}), s8[4194304]{0:T(1024)(128)(4,1)S(1)}, s32[]{:S(2)}) async-start(s8[4718592]{0:T(1024)(128)(4,1)} %bitcast.52), calls=%async_computation | async-start | bytes 8388608
  253.6 10.5 %slice-start.1 = ((s8[4718592]{0:T(1024)(128)(4,1)}), s8[524288]{0:T(1024)(128)(4,1)S(1)}, s32[]{:S(2)}) async-start(s8[4718592]{0:T(1024)(128)(4,1)} %bitcast.52), calls=%async_computation.1 | async-start | bytes 1048576
  264.2 5.4 %copy-start.1 = (f32[383,2,24,128]{3,0,1,2:T(8,128)S(1)}, f32[383,2,24,128]{3,0,1,2:T(8,128)}, u32[]{:S(2)}) copy-start(f32[383,2,24,128]{3,0,1,2:T(8,128)} %copy.29) | copy-start | bytes 28237828
  269.6 6.1 %copy-start.2 = (f32[384,1,24,128]{3,2,1,0:T(8,128)S(1)}, f32[384,1,24,128]{3,2,1,0:T(8,128)}, u32[]{:S(2)}) copy-start(f32[384,1,24,128]{3,2,1,0:T(8,128)} %get-tuple-element.12) | copy-start | bytes 14155780

commit v2 on v1

v2 whole, which is shorter than its diff:
```python
import functools
import math

import jax
import jax.numpy as jnp
from jax import lax
from jax.experimental import pallas as pl
from jax.experimental.pallas import tpu as pltpu
from jax.sharding import PartitionSpec as P

NLON = 768


def with_halo(array, sides, width):
    for axis, dim in sides:
        count, length = (lax.axis_size(axis), array.shape[dim])
        up = [(i, (i + 1) % count) for i in range(count - 1)]
        down = [(j, i) for i, j in up]
        last = lax.slice_in_dim(array, length - width, length, axis=dim)
        first = lax.slice_in_dim(array, 0, width, axis=dim)
        before = lax.ppermute(last, axis, up)
        after = lax.ppermute(first, axis, down)
        array = jnp.concatenate([before, array, after], axis=dim)
    return array


def wave_table(modes, count):
    columns = jnp.arange(count, dtype=jnp.int32)
    phase = modes[:, None] * columns[None, :] % count
    angle = phase.astype(jnp.float32) * (2.0 * math.pi / count)
    factor = count ** (-0.5)
    return jnp.stack([jnp.cos(angle) * factor, -jnp.sin(angle) * factor], axis=1)


def on_device(spec_in, legendre, mode_slot, w_in, b_in, w_out, kernel):
    high = lax.Precision.HIGHEST
    slots_here = legendre.shape[0]
    lat_index = lax.axis_index("lat")
    local_modes = lax.dynamic_slice_in_dim(mode_slot, lat_index * slots_here, slots_here)
    degrees = jnp.arange(legendre.shape[2], dtype=jnp.int32)
    masked = jnp.where(
        degrees[None, None, :] >= local_modes[:, None, None], legendre, jnp.float32(0.0)
    )
    waves = wave_table(mode_slot, NLON)
    coeff = jnp.einsum("sbcrl,stl->sbcrt", spec_in.astype(jnp.float32), masked, precision=high)
    grid = jnp.einsum(
        "sbcrt,srp->btcp",
        lax.all_to_all(coeff, "lat", split_axis=4, concat_axis=0, tiled=True),
        waves,
        precision=high,
    ).astype(jnp.bfloat16)
    batch, rows_here, chan_here, columns = grid.shape
    whole = lax.all_gather(grid, "chan", axis=2, tiled=True)
    chan_index = lax.axis_index("chan")
    w_local = lax.dynamic_slice_in_dim(w_out, chan_index * chan_here, chan_here, 0)
    pre = jnp.einsum("hc,btcp->bthp", w_in, whole, preferred_element_type=jnp.float32)
    hidden = jax.nn.gelu(pre + b_in[None, None, :, None], approximate=True).astype(jnp.bfloat16)
    branch = jnp.einsum("ch,bthp->btcp", w_local, hidden, preferred_element_type=jnp.float32)
    mixed = (grid.astype(jnp.float32) + branch).astype(jnp.bfloat16)
    half = columns // 2
    last_row = lax.axis_size("lat") - 1
    padded = with_halo(mixed, (("lat", 1),), 1)
    upper = jnp.where(lat_index == 0, jnp.roll(mixed[:, 0:1], half, axis=3), padded[:, 0:1])
    lower = jnp.where(lat_index == last_row, jnp.roll(mixed[:, -1:], half, axis=3), padded[:, -1:])
    stacked = jnp.concatenate([upper, padded[:, 1:-1], lower], axis=1).astype(jnp.float32)
    wide = mixed.astype(jnp.float32)
    conv = jnp.zeros_like(wide)
    for i in range(3):
        band = stacked[:, i : i + rows_here]
        for j in range(3):
            conv = conv + kernel[:, 3 * i + j][None, None, :, None] * jnp.roll(band, 1 - j, axis=3)
    field = wide + conv
    modes = jnp.einsum("btcp,srp->sbcrt", field, waves, precision=high)
    return jnp.einsum(
        "sbcrt,stl->sbcrl",
        lax.all_to_all(modes, "lat", split_axis=0, concat_axis=4, tiled=True),
        masked,
        precision=high,
    ).astype(jnp.bfloat16)


GROUP = 8
LANES = 128


def cosine(phase, count):
    phase = phase - jnp.floor((phase + 0.5) * (1.0 / count)) * count
    turn = jnp.abs(phase - 0.5 * count) - 0.25 * count
    x = turn * (2.0 * math.pi / count)
    y = x * x
    total = jnp.full_like(y, -1.0 / math.factorial(11))
    for power, sign in ((9, 1.0), (7, -1.0), (5, 1.0), (3, -1.0), (1, 1.0)):
        total = total * y + sign / math.factorial(power)
    return total * x


def rows_kernel(lats, chans, chunks, columns, mode_ref, spec_ref, legendre_ref, taps_ref,
                w_in_ref, b_in_ref, w_out_ref, field_ref, masked_ref,
                raw, table, stage, coeff, recv, send, got, mix, field, waves, waves_t, filters, perm, marks,
                raw_got, table_sent, field_sent, fwd_sent, fwd_got, bwd_sent, bwd_got):
    slots, span, degrees = raw.shape[1:]
    count = lats * chans
    rows, rows_all = span // count, span * chunks
    depth, width = coeff.shape[3:]
    groups = slots // GROUP
    pair = 2 * GROUP
    lat, chan = lax.axis_index("lat"), lax.axis_index("chan")
    me = lat * chans + chan
    bf16, f32 = jnp.bfloat16, jnp.float32
    across = (((1,), (1,)), ((), ()))

    def fetch(k):
        return pltpu.make_async_copy(
            legendre_ref.at[:, pl.ds(k * span, span), :], raw.at[k % 2], raw_got.at[k % 2])

    def store_table(k):
        part = pl.ds(k * span, span)
        return pltpu.make_async_copy(table.at[:, part, :], masked_ref.at[:, part, :], table_sent.at[k])

    def to_all(block, landing, here, send_sem, recv_sem):
        def to_peer(i, _):
            to = (me + i) % count
            pltpu.make_async_remote_copy(
                src_ref=block(to), dst_ref=landing, send_sem=send_sem, recv_sem=recv_sem,
                device_id=(to // chans, to % chans), device_id_type=pl.DeviceIdType.MESH,
            ).start()
            return 0

        pltpu.make_async_copy(block(me), here, recv_sem).start()
        lax.fori_loop(1, count, to_peer, 0)

    fetch(0).start()
    lane = lax.broadcasted_iota(jnp.int32, (span, degrees), 1)

    def forward(k, _):
        fetch(k).wait()

        @pl.when(k < chunks - 1)
        def _():
            fetch(k + 1).start()

        def group(g, _):
            for i in range(GROUP):
                s = g * GROUP + i
                least = mode_ref[lat * slots + s]
                block = jnp.where(lane >= least, raw[k % 2, s], 0.0).astype(bf16)
                table[s, pl.ds(pl.multiple_of(k * span, span), span), :] = block
                value = lax.dot_general(
                    block, spec_ref[s].reshape(2 * width, degrees), across,
                    preferred_element_type=f32)
                for r in range(2):
                    stage[pl.ds(r * GROUP + i, span, stride=pair), :] = value[:, r * width : (r + 1) * width]
            out = stage[...].astype(bf16).reshape(count, rows, pair, width)
            coeff[k, :, :, pl.ds(pl.multiple_of(g * pair, pair), pair), :] = out
            return 0

        lax.fori_loop(0, groups, group, 0)
        store_table(k).start()
        landing = recv.at[k, :, chan, pl.ds(lat * depth, depth), :]
        to_all(lambda to: coeff.at[k, to], landing, landing, fwd_sent, fwd_got.at[k])
        return 0

    lax.fori_loop(0, chunks, forward, 0)

    factor = columns ** -0.5
    size = lats * depth

    def mark(n, _):
        row = jnp.full((1, width), mode_ref[n], jnp.int32).astype(f32)
        for r in range(2):
            marks[pl.ds(n // GROUP * pair + r * GROUP + n % GROUP, 1), :] = row
        return 0

    lax.fori_loop(0, lats * slots, mark, 0)
    i = lax.broadcasted_iota(jnp.int32, perm.shape, 0)
    j = lax.broadcasted_iota(jnp.int32, perm.shape, 1)
    perm[...] = jnp.where(j == i % width * 2 + i // width, 1.0, 0.0).astype(bf16)

    def wave_rows(n, _):
        here = pl.ds(pl.multiple_of(n * LANES, LANES), LANES)
        k = lax.broadcasted_iota(jnp.int32, (LANES, columns), 0) + n * LANES
        p = lax.broadcasted_iota(jnp.int32, (LANES, columns), 1)
        quarter = (k // GROUP) % 2 * (columns // 4)
        phase = marks[here, :1] * p.astype(f32) + quarter.astype(f32)
        waves[here, :] = (cosine(phase, columns) * factor).astype(bf16)
        return 0

    lax.fori_loop(0, size // LANES, wave_rows, 0)

    line = jnp.concatenate(
        [jnp.transpose(marks[n * LANES : (n + 1) * LANES, :LANES])[:1] for n in range(size // LANES)], axis=1)

    def wave_columns(n, _):
        here = pl.ds(pl.multiple_of(n * LANES, LANES), LANES)
        p = lax.broadcasted_iota(jnp.int32, (LANES, size), 0) + n * LANES
        k = lax.broadcasted_iota(jnp.int32, (LANES, size), 1)
        quarter = (k // GROUP) % 2 * (columns // 4)
        phase = line * p.astype(f32) + quarter.astype(f32)
        waves_t[here, :] = (cosine(phase, columns) * factor).astype(bf16)
        return 0

    lax.fori_loop(0, columns // LANES, wave_columns, 0)

    angle = jnp.concatenate(
        [marks[pl.ds(lat * depth + g * pair, GROUP), :] for g in range(groups)], axis=0)
    cos, minus_sin = cosine(angle, columns), cosine(angle + 0.25 * columns, columns)
    for i in range(3):
        left, here, right = (taps_ref[3 * i + j : 3 * i + j + 1, :] for j in range(3))
        filters[2 * i] = here + (left + right) * cos + (1.0 if i == 1 else 0.0)
        filters[2 * i + 1] = (left - right) * minus_sin
    filters[6] = cosine(angle * (columns // 2), columns)

    def one_chunk(k, _):
        pltpu.make_async_copy(recv.at[k], recv.at[k], fwd_got.at[k]).wait()

        def one_row(j, _):
            merged = jnp.concatenate([recv[k, j, i] for i in range(chans)], axis=1)
            grid = jnp.dot(waves_t[...], merged, preferred_element_type=f32).astype(bf16)
            pre = lax.dot_general(grid, w_in_ref[...], across, preferred_element_type=f32) + b_in_ref[...]
            hidden = jax.nn.gelu(pre, approximate=True).astype(bf16)
            branch = lax.dot_general(hidden, w_out_ref[...], across, preferred_element_type=f32)
            mixed = (grid.astype(f32) + branch).astype(bf16)
            modes = jnp.dot(waves[...], mixed, preferred_element_type=f32).astype(bf16)
            for i in range(chans):
                send[k, j, i] = modes[:, i * width : (i + 1) * width]
            return 0

        lax.fori_loop(0, rows, one_row, 0)
        landing = got.at[pl.ds(1 + k * span + me * rows, rows)]
        to_all(
            lambda to: send.at[k, :, to % chans, pl.ds((to // chans) * depth, depth), :],
            landing, landing, bwd_sent, bwd_got.at[k])
        return 0

    lax.fori_loop(0, chunks, one_chunk, 0)

    most = mix.shape[0] // pair
    lag = most - span
    copies = []
    for k in range(chunks):
        arrived = got.at[pl.ds(1 + k * span, span)]
        pltpu.make_async_copy(arrived, arrived, bwd_got.at[k]).wait()
        low = max(k * span - lag, 0)
        high = rows_all if k == chunks - 1 else (k + 1) * span - lag

        def group(g, _):
            part = pl.ds(pl.multiple_of(g * pair, pair), pair)
            own = pl.ds(pl.multiple_of(g * GROUP, GROUP), GROUP)
            fs = [filters[i, own, :] for i in range(7)]

            def load(t):
                both = got[t, part, :].astype(f32)
                return both[:GROUP], both[GROUP:]

            both_signs = jnp.concatenate([fs[6], fs[6]], axis=0)
            if k == 0:
                got[0, part, :] = (got[1, part, :].astype(f32) * both_signs).astype(bf16)
            if k == chunks - 1:
                got[rows_all + 1, part, :] = (got[rows_all, part, :].astype(f32) * both_signs).astype(bf16)

            def some_rows(n, held):
                for u in range(GROUP):
                    t = n * GROUP + u
                    three = (*held, load(low + t + 2))
                    real = imag = 0.0
                    for i, (x, y) in enumerate(three):
                        real = real + fs[2 * i] * x - fs[2 * i + 1] * y
                        imag = imag + fs[2 * i] * y + fs[2 * i + 1] * x
                    mix[pl.ds(t, GROUP, stride=most), :] = real
                    mix[pl.ds(GROUP * most + t, GROUP, stride=most), :] = imag
                    held = three[1:]
                return held

            lax.fori_loop(0, (high - low) // GROUP, some_rows, (load(low), load(low + 1)))
            for i in range(GROUP):
                parts = [mix[pl.ds((r * GROUP + i) * most, high - low), :] for r in range(2)]
                both = jnp.concatenate(parts, axis=1).astype(bf16)
                field[g * GROUP + i, low:high, :] = jnp.dot(
                    both, perm[...], preferred_element_type=f32).astype(bf16)
            return 0

        lax.fori_loop(0, groups, group, 0)
        copy = pltpu.make_async_copy(
            field.at[:, low:high, :], field_ref.at[:, low:high, :], field_sent.at[k])
        copy.start()
        copies.append(copy)

    for k, copy in enumerate(copies):
        copy.wait()
        store_table(k).wait()
    for ref, sem in ((coeff, fwd_sent), (coeff, bwd_sent)):
        away = ref.at[:, pl.ds(0, count - 1)]
        pltpu.make_async_copy(away, away, sem).wait()


def degrees_kernel(field_ref, masked_ref, out_ref):
    for s in range(field_ref.shape[0]):
        out = lax.dot_general(
            field_ref[s], masked_ref[s], (((0,), (0,)), ((), ())), preferred_element_type=jnp.float32)
        out_ref[s] = out.astype(jnp.bfloat16).reshape(out_ref.shape[1:])


def on_device_rows(spec_in, legendre, mode_slot, w_in, b_in, w_out, kernel):
    lats, chans = lax.axis_size("lat"), lax.axis_size("chan")
    count = lats * chans
    slots, rows_all, degrees = legendre.shape
    width = spec_in.shape[2]
    own_rows = rows_all // count
    chunks = next(k for k in (4, 3, 2, 1) if own_rows % k == 0 and rows_all // k % 16 == 0)
    rows, span = own_rows // chunks, rows_all // chunks
    columns, groups, depth = NLON, slots // GROUP, 2 * slots
    hbm, vmem = pl.BlockSpec(memory_space=pl.ANY), pl.BlockSpec(memory_space=pltpu.VMEM)
    smem = pl.BlockSpec(memory_space=pltpu.SMEM)
    lag = 16 if chunks > 1 else 0
    bf16, f32 = jnp.bfloat16, jnp.float32
    field, masked = pl.pallas_call(
        functools.partial(rows_kernel, lats, chans, chunks, columns),
        out_shape=(
            jax.ShapeDtypeStruct((slots, rows_all, 2 * width), bf16),
            jax.ShapeDtypeStruct((slots, rows_all, degrees), bf16),
        ),
        in_specs=[smem, vmem, hbm] + [vmem] * 4,
        out_specs=(hbm, hbm),
        scratch_shapes=[
            pltpu.VMEM((2, slots, span, degrees), f32),
            pltpu.VMEM((slots, rows_all, degrees), bf16),
            pltpu.VMEM((span * 2 * GROUP, width), f32),
            pltpu.VMEM((chunks, count, rows, depth, width), bf16),
            pltpu.VMEM((chunks, rows, chans, lats * depth, width), bf16),
            pltpu.VMEM((chunks, rows, chans, lats * depth, width), bf16),
            pltpu.VMEM((rows_all + 2, depth, width), bf16),
            pltpu.VMEM(((span + lag) * 2 * GROUP, width), f32),
            pltpu.VMEM((slots, rows_all, 2 * width), bf16),
            pltpu.VMEM((lats * depth, columns), bf16),
            pltpu.VMEM((columns, lats * depth), bf16),
            pltpu.VMEM((7, slots, width), f32),
            pltpu.VMEM((2 * width, 2 * width), bf16),
            pltpu.VMEM((lats * depth, width), f32),
            pltpu.SemaphoreType.DMA((2,)),
            pltpu.SemaphoreType.DMA((chunks,)),
            pltpu.SemaphoreType.DMA((chunks,)),
            pltpu.SemaphoreType.DMA,
            pltpu.SemaphoreType.DMA((chunks,)),
            pltpu.SemaphoreType.DMA,
            pltpu.SemaphoreType.DMA((chunks,)),
        ],
        compiler_params=pltpu.CompilerParams(vmem_limit_bytes=61 * 1024 * 1024, has_side_effects=True),
        name="rows",
    )(mode_slot, jnp.swapaxes(spec_in[:, 0], 1, 2), legendre, kernel.T, w_in, b_in[None, :], w_out)
    some = next(n for n in (4, 3, 2, 1) if slots % n == 0)
    out = pl.pallas_call(
        degrees_kernel,
        grid=(slots // some,),
        out_shape=jax.ShapeDtypeStruct((slots, width, 2, degrees), bf16),
        in_specs=[
            pl.BlockSpec((some, rows_all, 2 * width), lambda n: (n, 0, 0)),
            pl.BlockSpec((some, rows_all, degrees), lambda n: (n, 0, 0)),
        ],
        out_specs=pl.BlockSpec((some, width, 2, degrees), lambda n: (n, 0, 0, 0)),
        compiler_params=pltpu.CompilerParams(vmem_limit_bytes=61 * 1024 * 1024),
        name="degrees",
    )(field, masked)
    return out[:, None]


def solution(mesh):
    in_specs = (
        P("lat", None, "chan", None, None),
        P("lat", None, None),
        P(),
        P(),
        P(),
        P(),
        P("chan", None),
    )
    out_specs = P("lat", None, "chan", None, None)
    count = mesh.shape["lat"] * mesh.shape["chan"]

    def call(spec_in, legendre, *rest):
        samples, rows_all = spec_in.shape[1], legendre.shape[1]
        slots = spec_in.shape[0] // mesh.shape["lat"]
        by_rows = samples == 1 and rows_all % count == 0 and slots % GROUP == 0
        body = on_device_rows if by_rows else on_device
        return jax.shard_map(
            body, mesh=mesh, in_specs=in_specs, out_specs=out_specs, check_vma=False
        )(spec_in, legendre, *rest)

    return call
```

time: 302 us -> 238 us (0.79)
  local copies, waits for them, and re-layouts: 53.7 us -> 5.58 us
  Pallas kernels: 212 us -> 232 us
  other arithmetic: 18.9 us -> 0 us
  matrix products: 16.3 us -> 0 us
    pallas_call x1 -> x2, Pallas kernels: 212 us -> 232 us  [the longest x1 222 us: on_device_rows(): pl.pallas_call(functools.partial(rows_kernel, lats, chans, chunks, column...]
    another operation x4 -> x0, other arithmetic: 16.9 us -> none  [the longest x3 16.8 us: call(): jax.shard_map(body, mesh=mesh, in_specs=in_specs, out_specs=out_specs, ch...]
    dot_general x2 -> x0, matrix products: 16.3 us -> none  [the longest x1 8.33 us: on_device_rows(): jnp.einsum('scrl,stl->trsc', spec_in[:, 0], masked, preferred_element_typ...]
    slice x3 -> x0, local copies, waits for them, and re-layouts: 15.5 us -> none  [the longest x2 12.4 us: on_device_rows(): below = jnp.concatenate([modes[1:], modes[-1:] * sign], axis=0)]
    unnamed x20 -> x1, local copies, waits for them, and re-layouts: 19.9 us -> 5.58 us
    broadcast_in_dim x1 -> x0, local copies, waits for them, and re-layouts: 12.4 us -> none  [on_device_rows(): return out.astype(jnp.bfloat16)[:, None]]
    convert_element_type x1 -> x0, local copies, waits for them, and re-layouts: 5.22 us -> none  [on_device_rows(): coeff.astype(jnp.bfloat16).reshape(chunks, count, rows, 2 * slots, width)]
where the time goes in v2:
time: 238 us; the launch traced here: 237 us
  Pallas kernels  232 us (97%)
  local copies, waits for them, and re-layouts  5.58 us (2%)
    pallas_call x1, Pallas kernels, on_device_rows(): pl.pallas_call(functools.partial(rows_kernel, lats, chans, chunks, column...  222 us
    pallas_call x1, Pallas kernels, on_device_rows(): pl.pallas_call(degrees_kernel, grid=(slots // some,), out_shape=jax.Shape...  9.4 us
    unnamed x1, local copies, waits for them, and re-layouts  5.58 us

profile of v2, /device:TPU:11, one launch (start us, length us, event | category | flops | bytes accessed | tf_op | source)
XLA Modules:
  0.0 237.4 jit_solution(3084211905839265715)
XLA Ops:
  0.0 5.6 %copy.11 = bf16[24,1,128,2,384]{4,2,3,0,1:T(8,128)(2,1)} copy(bf16[24,1,128,2,384]{4,3,2,1,0:T(2,128)(2,1)} %param.7) | data formatting | bytes 9437184 | tf_op args[0]
  5.6 222.4 %rows.1 = (bf16[24,384,256]{2,1,0:T(8,128)(2,1)}, bf16[24,384,384]{2,1,0:T(8,128)(2,1)}) custom-call(s32[384]{0:T(512)} %mode_ref.1, bf16[24,2,128,384]{3,2,1,0:T(8,128)(2,1)} %bitcast.10, f32[24,384,384]{2,1,0:T(8,128)} %legendre_ref.1, f32[9,128]{1,0:T(8,128)} %bitcast.11, bf16[512,256]{1,0:T(8,128)(2,1)} %w_in_ref.1, f32[1,512]{1,0:T(1,128)} %bitcast.12, ...), custom_call_target="tpu_custom_call" | custom-call | tf_op jit(solution)/shard_map/rows/pallas_call | solution.py:316
  228.0 9.4 %degrees.1 = bf16[24,128,2,384]{3,2,1,0:T(2,128)(2,1)} custom-call(bf16[24,384,256]{2,1,0:T(8,128)(2,1)} %get-tuple-element.7.field_ref, bf16[24,384,384]{2,1,0:T(8,128)(2,1)} %get-tuple-element.8.masked_ref), custom_call_target="tpu_custom_call" | custom-call | tf_op jit(solution)/shard_map/degrees/pallas_call | solution.py:351

commit v3 on v2

--- a/solution.py
+++ b/solution.py
@@ -95,10 +95,11 @@
 
 
 def rows_kernel(lats, chans, chunks, columns, mode_ref, spec_ref, legendre_ref, taps_ref,
-                w_in_ref, b_in_ref, w_out_ref, field_ref, masked_ref,
-                raw, table, stage, coeff, recv, send, got, mix, field, waves, waves_t, filters, perm, marks,
-                raw_got, table_sent, field_sent, fwd_sent, fwd_got, bwd_sent, bwd_got):
-    slots, span, degrees = raw.shape[1:]
+                w_in_ref, b_in_ref, w_out_ref, out_ref,
+                raw, spec, table, stage, coeff, recv, send, got, mix, field, waves, waves_t, filters, perm, perm_t, marks,
+                raw_got, spec_got, out_sent, fwd_sent, fwd_got, bwd_sent, bwd_got):
+    span, degrees = raw.shape[2:]
+    slots = table.shape[0]
     count = lats * chans
     rows, rows_all = span // count, span * chunks
     depth, width = coeff.shape[3:]
@@ -109,13 +110,14 @@
     bf16, f32 = jnp.bfloat16, jnp.float32
     across = (((1,), (1,)), ((), ()))
 
-    def fetch(k):
+    def fetch(n):
         return pltpu.make_async_copy(
-            legendre_ref.at[:, pl.ds(k * span, span), :], raw.at[k % 2], raw_got.at[k % 2])
-
-    def store_table(k):
-        part = pl.ds(k * span, span)
-        return pltpu.make_async_copy(table.at[:, part, :], masked_ref.at[:, part, :], table_sent.at[k])
+            legendre_ref.at[pl.ds(n % groups * GROUP, GROUP), pl.ds(n // groups * span, span), :],
+            raw.at[n % 2], raw_got.at[n % 2])
+
+    def fetch_spec(g):
+        part = pl.ds(g * GROUP, GROUP)
+        return pltpu.make_async_copy(spec_ref.at[part], spec.at[part], spec_got.at[g])
 
     def to_all(block, landing, here, send_sem, recv_sem):
         def to_peer(i, _):
@@ -130,37 +132,52 @@
         lax.fori_loop(1, count, to_peer, 0)
 
     fetch(0).start()
+    for g in range(groups):
+        fetch_spec(g).start()
+    i = lax.broadcasted_iota(jnp.int32, perm.shape, 0)
+    j = lax.broadcasted_iota(jnp.int32, perm.shape, 1)
+    perm[...] = jnp.where(j == i % width * 2 + i // width, 1.0, 0.0).astype(bf16)
+    perm_t[...] = jnp.where(i == j % width * 2 + j // width, 1.0, 0.0).astype(bf16)
     lane = lax.broadcasted_iota(jnp.int32, (span, degrees), 1)
 
-    def forward(k, _):
-        fetch(k).wait()
-
-        @pl.when(k < chunks - 1)
-        def _():
-            fetch(k + 1).start()
-
-        def group(g, _):
-            for i in range(GROUP):
-                s = g * GROUP + i
-                least = mode_ref[lat * slots + s]
-                block = jnp.where(lane >= least, raw[k % 2, s], 0.0).astype(bf16)
-                table[s, pl.ds(pl.multiple_of(k * span, span), span), :] = block
-                value = lax.dot_general(
-                    block, spec_ref[s].reshape(2 * width, degrees), across,
-                    preferred_element_type=f32)
-                for r in range(2):
-                    stage[pl.ds(r * GROUP + i, span, stride=pair), :] = value[:, r * width : (r + 1) * width]
-            out = stage[...].astype(bf16).reshape(count, rows, pair, width)
-            coeff[k, :, :, pl.ds(pl.multiple_of(g * pair, pair), pair), :] = out
-            return 0
-
-        lax.fori_loop(0, groups, group, 0)
-        store_table(k).start()
-        landing = recv.at[k, :, chan, pl.ds(lat * depth, depth), :]
-        to_all(lambda to: coeff.at[k, to], landing, landing, fwd_sent, fwd_got.at[k])
+    def forward(n, _):
+        k, g = n // groups, n % groups
+        fetch(n).wait()
+
+        @pl.when(n < chunks * groups - 1)
+        def _():
+            fetch(n + 1).start()
+
+        @pl.when(k == 0)
+        def _():
+            fetch_spec(g).wait()
+
+        for i in range(GROUP):
+            s = g * GROUP + i
+            least = mode_ref[lat * slots + s]
+            block = jnp.where(lane >= least, raw[n % 2, i], 0.0).astype(bf16)
+            table[s, pl.ds(pl.multiple_of(k * span, span), span), :] = block
+            value = lax.dot_general(
+                block, spec[s].reshape(2 * width, degrees), across, preferred_element_type=f32)
+            value = jnp.dot(value.astype(bf16), perm_t[...], preferred_element_type=f32)
+            for r in range(2):
+                stage[pl.ds(r * GROUP + i, span, stride=pair), :] = value[:, r * width : (r + 1) * width]
+        part = pl.ds(pl.multiple_of(g * pair, pair), pair)
+        coeff[k, :, :, part, :] = stage[...].astype(bf16).reshape(count, rows, pair, width)
+
+        @pl.when(k == 0)
+        def _():
+            landing = recv.at[k, :, chan, pl.ds(lat * depth + g * pair, pair), :]
+            to_all(lambda to: coeff.at[k, to, :, part, :], landing, landing, fwd_sent, fwd_got.at[k])
+
+        @pl.when((k > 0) & (g == groups - 1))
+        def _():
+            landing = recv.at[k, :, chan, pl.ds(lat * depth, depth), :]
+            to_all(lambda to: coeff.at[k, to], landing, landing, fwd_sent, fwd_got.at[k])
+
         return 0
 
-    lax.fori_loop(0, chunks, forward, 0)
+    lax.fori_loop(0, chunks * groups, forward, 0)
 
     factor = columns ** -0.5
     size = lats * depth
@@ -172,10 +189,6 @@
         return 0
 
     lax.fori_loop(0, lats * slots, mark, 0)
-    i = lax.broadcasted_iota(jnp.int32, perm.shape, 0)
-    j = lax.broadcasted_iota(jnp.int32, perm.shape, 1)
-    perm[...] = jnp.where(j == i % width * 2 + i // width, 1.0, 0.0).astype(bf16)
-
     def wave_rows(n, _):
         here = pl.ds(pl.multiple_of(n * LANES, LANES), LANES)
         k = lax.broadcasted_iota(jnp.int32, (LANES, columns), 0) + n * LANES
@@ -226,25 +239,49 @@
             return 0
 
         lax.fori_loop(0, rows, one_row, 0)
-        landing = got.at[pl.ds(1 + k * span + me * rows, rows)]
-        to_all(
-            lambda to: send.at[k, :, to % chans, pl.ds((to // chans) * depth, depth), :],
-            landing, landing, bwd_sent, bwd_got.at[k])
+        landing = pl.ds(1 + k * span + me * rows, rows)
+
+        @pl.when(k < chunks - 1)
+        def _():
+            here = got.at[landing]
+            to_all(
+                lambda to: send.at[k, :, to % chans, pl.ds((to // chans) * depth, depth), :],
+                here, here, bwd_sent, bwd_got.at[k])
+
+        @pl.when(k == chunks - 1)
+        def _():
+            def group(g, _):
+                here = got.at[landing, pl.ds(g * pair, pair), :]
+                to_all(
+                    lambda to: send.at[k, :, to % chans, pl.ds((to // chans) * depth + g * pair, pair), :],
+                    here, here, bwd_sent, bwd_got.at[k + g])
+                return 0
+
+            lax.fori_loop(0, groups, group, 0)
+
         return 0
 
     lax.fori_loop(0, chunks, one_chunk, 0)
 
     most = mix.shape[0] // pair
     lag = most - span
-    copies = []
+
+    def result(g):
+        part = pl.ds(g * GROUP, GROUP)
+        return pltpu.make_async_copy(spec.at[part], out_ref.at[part], out_sent.at[g])
+
     for k in range(chunks):
-        arrived = got.at[pl.ds(1 + k * span, span)]
-        pltpu.make_async_copy(arrived, arrived, bwd_got.at[k]).wait()
+        arrived = pl.ds(1 + k * span, span)
+        if k < chunks - 1:
+            pltpu.make_async_copy(got.at[arrived], got.at[arrived], bwd_got.at[k]).wait()
         low = max(k * span - lag, 0)
         high = rows_all if k == chunks - 1 else (k + 1) * span - lag
 
         def group(g, _):
             part = pl.ds(pl.multiple_of(g * pair, pair), pair)
+            if k == chunks - 1:
+                last = got.at[arrived, part, :]
+                pltpu.make_async_copy(last, last, bwd_got.at[k + g]).wait()
             own = pl.ds(pl.multiple_of(g * GROUP, GROUP), GROUP)
             fs = [filters[i, own, :] for i in range(7)]
 
@@ -277,27 +314,36 @@
                 both = jnp.concatenate(parts, axis=1).astype(bf16)
                 field[g * GROUP + i, low:high, :] = jnp.dot(
                     both, perm[...], preferred_element_type=f32).astype(bf16)
+            if k == chunks - 1:
+                for i in range(GROUP):
+                    s = g * GROUP + i
+                    out = lax.dot_general(
+                        field[s], table[s], (((0,), (0,)), ((), ())), preferred_element_type=f32)
+                    spec[s] = out.astype(bf16).reshape(spec.shape[1:])
+                result(g).start()
             return 0
 
         lax.fori_loop(0, groups, group, 0)
-        copy = pltpu.make_async_copy(
-            field.at[:, low:high, :], field_ref.at[:, low:high, :], field_sent.at[k])
-        copy.start()
-        copies.append(copy)
-
-    for k, copy in enumerate(copies):
-        copy.wait()
-        store_table(k).wait()
+
+    for g in range(groups):
+        result(g).wait()
     for ref, sem in ((coeff, fwd_sent), (coeff, bwd_sent)):
         away = ref.at[:, pl.ds(0, count - 1)]
         pltpu.make_async_copy(away, away, sem).wait()
 
 
-def degrees_kernel(field_ref, masked_ref, out_ref):
-    for s in range(field_ref.shape[0]):
-        out = lax.dot_general(
-            field_ref[s], masked_ref[s], (((0,), (0,)), ((), ())), preferred_element_type=jnp.float32)
-        out_ref[s] = out.astype(jnp.bfloat16).reshape(out_ref.shape[1:])
+def hand_on(pieces, in_ref, out_ref, held, got, sent):
+    size = in_ref.shape[0] // pieces
+    parts = [pl.ds(i * size, size) for i in range(pieces)]
+    inward = [pltpu.make_async_copy(in_ref.at[p], held.at[p], got.at[i]) for i, p in enumerate(parts)]
+    outward = [pltpu.make_async_copy(held.at[p], out_ref.at[p], sent.at[i]) for i, p in enumerate(parts)]
+    for copy in inward:
+        copy.start()
+    for before, after in zip(inward, outward):
+        before.wait()
+        after.start()
+    for copy in outward:
+        copy.wait()
 
 
 def on_device_rows(spec_in, legendre, mode_slot, w_in, b_in, w_out, kernel):
@@ -313,16 +359,14 @@
     smem = pl.BlockSpec(memory_space=pltpu.SMEM)
     lag = 16 if chunks > 1 else 0
     bf16, f32 = jnp.bfloat16, jnp.float32
-    field, masked = pl.pallas_call(
+    out = pl.pallas_call(
         functools.partial(rows_kernel, lats, chans, chunks, columns),
-        out_shape=(
-            jax.ShapeDtypeStruct((slots, rows_all, 2 * width), bf16),
-            jax.ShapeDtypeStruct((slots, rows_all, degrees), bf16),
-        ),
-        in_specs=[smem, vmem, hbm] + [vmem] * 4,
-        out_specs=(hbm, hbm),
+        out_shape=jax.ShapeDtypeStruct((slots, width, 2, degrees), bf16),
+        in_specs=[smem] + [hbm] * 2 + [vmem] * 4,
+        out_specs=hbm,
         scratch_shapes=[
-            pltpu.VMEM((2, slots, span, degrees), f32),
+            pltpu.VMEM((2, GROUP, span, degrees), f32),
+            pltpu.VMEM((slots, width, 2, degrees), bf16),
             pltpu.VMEM((slots, rows_all, degrees), bf16),
             pltpu.VMEM((span * 2 * GROUP, width), f32),
             pltpu.VMEM((chunks, count, rows, depth, width), bf16),
@@ -335,31 +379,33 @@
             pltpu.VMEM((columns, lats * depth), bf16),
             pltpu.VMEM((7, slots, width), f32),
             pltpu.VMEM((2 * width, 2 * width), bf16),
+            pltpu.VMEM((2 * width, 2 * width), bf16),
             pltpu.VMEM((lats * depth, width), f32),
             pltpu.SemaphoreType.DMA((2,)),
-            pltpu.SemaphoreType.DMA((chunks,)),
-            pltpu.SemaphoreType.DMA((chunks,)),
+            pltpu.SemaphoreType.DMA((groups,)),
+            pltpu.SemaphoreType.DMA((groups,)),
             pltpu.SemaphoreType.DMA,
             pltpu.SemaphoreType.DMA((chunks,)),
             pltpu.SemaphoreType.DMA,
-            pltpu.SemaphoreType.DMA((chunks,)),
+            pltpu.SemaphoreType.DMA((chunks + groups - 1,)),
         ],
         compiler_params=pltpu.CompilerParams(vmem_limit_bytes=61 * 1024 * 1024, has_side_effects=True),
         name="rows",
-    )(mode_slot, jnp.swapaxes(spec_in[:, 0], 1, 2), legendre, kernel.T, w_in, b_in[None, :], w_out)
-    some = next(n for n in (4, 3, 2, 1) if slots % n == 0)
+    )(mode_slot, spec_in[:, 0], legendre, kernel.T, w_in, b_in[None, :], w_out)
+    pieces = next(n for n in (8, 6, 4, 3, 2, 1) if slots % n == 0)
     out = pl.pallas_call(
-        degrees_kernel,
-        grid=(slots // some,),
-        out_shape=jax.ShapeDtypeStruct((slots, width, 2, degrees), bf16),
-        in_specs=[
-            pl.BlockSpec((some, rows_all, 2 * width), lambda n: (n, 0, 0)),
-            pl.BlockSpec((some, rows_all, degrees), lambda n: (n, 0, 0)),
+        functools.partial(hand_on, pieces),
+        out_shape=jax.ShapeDtypeStruct(out.shape, bf16),
+        in_specs=[hbm],
+        out_specs=hbm,
+        scratch_shapes=[
+            pltpu.VMEM(out.shape, bf16),
+            pltpu.SemaphoreType.DMA((pieces,)),
+            pltpu.SemaphoreType.DMA((pieces,)),
         ],
-        out_specs=pl.BlockSpec((some, width, 2, degrees), lambda n: (n, 0, 0, 0)),
         compiler_params=pltpu.CompilerParams(vmem_limit_bytes=61 * 1024 * 1024),
-        name="degrees",
-    )(field, masked)
+        name="hand_on",
+    )(out)
     return out[:, None]
 
 

time: 238 us -> 225 us (0.945)
  Pallas kernels: 232 us -> 224 us
  local copies, waits for them, and re-layouts: 5.58 us -> 0 us
    unnamed x1 -> x0, local copies, waits for them, and re-layouts: 5.58 us -> none
    pallas_call x1, Pallas kernels: 9.4 us -> 4.12 us  [on_device_rows(): pl.pallas_call(functools.partial(hand_on, pieces), out_shape=jax.ShapeDty...]
where the time goes in v3:
time: 225 us; the launch traced here: 224 us
  Pallas kernels  224 us (100%)
    pallas_call x1, Pallas kernels, on_device_rows(): pl.pallas_call(functools.partial(rows_kernel, lats, chans, chunks, column...  220 us

profile of v3, /device:TPU:11, one launch (start us, length us, event | category | flops | bytes accessed | tf_op | source)
XLA Modules:
  0.0 224.5 jit_solution(16221197292925682916)
XLA Ops:
  0.0 220.4 %rows.1.in_ref = bf16[24,128,2,384]{3,2,1,0:T(2,128)(2,1)} custom-call(s32[384]{0:T(512)} %mode_ref.1, bf16[24,128,2,384]{3,2,1,0:T(2,128)(2,1)} %bitcast.6, f32[24,384,384]{2,1,0:T(8,128)} %legendre_ref.1, f32[9,128]{1,0:T(8,128)} %bitcast.7, bf16[512,256]{1,0:T(8,128)(2,1)} %w_in_ref.1, f32[1,512]{1,0:T(1,128)} %bitcast.8, bf16[256,512]{1,0:T(8,128)(2,1)} %w_out_ref.1), custom_call_target="tpu_custom_call" | custom-call | tf_op jit(solution)/shard_map/rows/pallas_call | solution.py:362
  220.4 4.1 %hand_on.1 = bf16[24,128,2,384]{3,2,1,0:T(2,128)(2,1)} custom-call(bf16[24,128,2,384]{3,2,1,0:T(2,128)(2,1)} %rows.1.in_ref), custom_call_target="tpu_custom_call" | custom-call | tf_op jit(solution)/shard_map/hand_on/pallas_call | solution.py:396

commit v4 on v3

--- a/solution.py
+++ b/solution.py
@@ -131,6 +131,15 @@
         pltpu.make_async_copy(block(me), here, recv_sem).start()
         lax.fori_loop(1, count, to_peer, 0)
 
+    barrier = pltpu.get_barrier_semaphore()
+
+    def greet(i, _):
+        to = (me + i) % count
+        pl.semaphore_signal(
+            barrier, inc=1, device_id=(to // chans, to % chans), device_id_type=pl.DeviceIdType.MESH)
+        return 0
+
+    lax.fori_loop(1, count, greet, 0)
     fetch(0).start()
     for g in range(groups):
         fetch_spec(g).start()
@@ -140,7 +149,7 @@
     perm_t[...] = jnp.where(i == j % width * 2 + j // width, 1.0, 0.0).astype(bf16)
     lane = lax.broadcasted_iota(jnp.int32, (span, degrees), 1)
 
-    def forward(n, _):
+    def work_out(n):
         k, g = n // groups, n % groups
         fetch(n).wait()
 
@@ -165,10 +174,22 @@
         part = pl.ds(pl.multiple_of(g * pair, pair), pair)
         coeff[k, :, :, part, :] = stage[...].astype(bf16).reshape(count, rows, pair, width)
 
+    def send_group(g):
+        part = pl.ds(g * pair, pair)
+        landing = recv.at[0, :, chan, pl.ds(lat * depth + g * pair, pair), :]
+        to_all(lambda to: coeff.at[0, to, :, part, :], landing, landing, fwd_sent, fwd_got.at[0])
+
+    work_out(0)
+    pl.semaphore_wait(barrier, count - 1)
+    send_group(0)
+
+    def forward(n, _):
+        k, g = n // groups, n % groups
+        work_out(n)
+
         @pl.when(k == 0)
         def _():
-            landing = recv.at[k, :, chan, pl.ds(lat * depth + g * pair, pair), :]
-            to_all(lambda to: coeff.at[k, to, :, part, :], landing, landing, fwd_sent, fwd_got.at[k])
+            send_group(g)
 
         @pl.when((k > 0) & (g == groups - 1))
         def _():
@@ -177,7 +198,7 @@
 
         return 0
 
-    lax.fori_loop(0, chunks * groups, forward, 0)
+    lax.fori_loop(1, chunks * groups, forward, 0)
 
     factor = columns ** -0.5
     size = lats * depth
@@ -389,7 +410,7 @@
             pltpu.SemaphoreType.DMA,
             pltpu.SemaphoreType.DMA((chunks + groups - 1,)),
         ],
-        compiler_params=pltpu.CompilerParams(vmem_limit_bytes=61 * 1024 * 1024, has_side_effects=True),
+        compiler_params=pltpu.CompilerParams(vmem_limit_bytes=61 * 1024 * 1024, has_side_effects=True, collective_id=0),
         name="rows",
     )(mode_slot, spec_in[:, 0], legendre, kernel.T, w_in, b_in[None, :], w_out)
     pieces = next(n for n in (8, 6, 4, 3, 2, 1) if slots % n == 0)

time: 225 us -> 220 us (0.978)
  Pallas kernels: 224 us -> 219 us
    pallas_call x1, Pallas kernels: 220 us -> 215 us  [on_device_rows(): pl.pallas_call(functools.partial(rows_kernel, lats, chans, chunks, column...]
where the time goes in v4:
time: 220 us; the launch traced here: 219 us
  Pallas kernels  219 us (100%)
    pallas_call x1, Pallas kernels, on_device_rows(): pl.pallas_call(functools.partial(rows_kernel, lats, chans, chunks, column...  215 us

profile of v4, /device:TPU:11, one launch (start us, length us, event | category | flops | bytes accessed | tf_op | source)
XLA Modules:
  0.0 219.1 jit_solution(18209666366000406525)
XLA Ops:
  0.0 215.0 %rows.1.in_ref = bf16[24,128,2,384]{3,2,1,0:T(2,128)(2,1)} custom-call(s32[384]{0:T(512)} %mode_ref.1, bf16[24,128,2,384]{3,2,1,0:T(2,128)(2,1)} %bitcast.6, f32[24,384,384]{2,1,0:T(8,128)} %legendre_ref.1, f32[9,128]{1,0:T(8,128)} %bitcast.7, bf16[512,256]{1,0:T(8,128)(2,1)} %w_in_ref.1, f32[1,512]{1,0:T(1,128)} %bitcast.8, bf16[256,512]{1,0:T(8,128)(2,1)} %w_out_ref.1), custom_call_target="tpu_custom_call" | custom-call | tf_op jit(solution)/shard_map/rows/pallas_call | solution.py:383
  215.0 4.1 %hand_on.1 = bf16[24,128,2,384]{3,2,1,0:T(2,128)(2,1)} custom-call(bf16[24,128,2,384]{3,2,1,0:T(2,128)(2,1)} %rows.1.in_ref), custom_call_target="tpu_custom_call" | custom-call | tf_op jit(solution)/shard_map/hand_on/pallas_call | solution.py:417

commit v5 on v4

--- a/solution.py
+++ b/solution.py
@@ -97,7 +97,7 @@
 def rows_kernel(lats, chans, chunks, columns, mode_ref, spec_ref, legendre_ref, taps_ref,
                 w_in_ref, b_in_ref, w_out_ref, out_ref,
                 raw, spec, table, stage, coeff, recv, send, got, mix, field, waves, waves_t, filters, perm, perm_t, marks,
-                raw_got, spec_got, out_sent, fwd_sent, fwd_got, bwd_sent, bwd_got):
+                raw_got, spec_got, fwd_sent, fwd_got, bwd_sent, bwd_got):
     span, degrees = raw.shape[2:]
     slots = table.shape[0]
     count = lats * chans
@@ -287,10 +287,6 @@
     most = mix.shape[0] // pair
     lag = most - span
 
-    def result(g):
-        part = pl.ds(g * GROUP, GROUP)
-        return pltpu.make_async_copy(spec.at[part], out_ref.at[part], out_sent.at[g])
-
     for k in range(chunks):
         arrived = pl.ds(1 + k * span, span)
         if k < chunks - 1:
@@ -340,31 +336,13 @@
                     s = g * GROUP + i
                     out = lax.dot_general(
                         field[s], table[s], (((0,), (0,)), ((), ())), preferred_element_type=f32)
-                    spec[s] = out.astype(bf16).reshape(spec.shape[1:])
-                result(g).start()
+                    out_ref[s] = out.astype(bf16).reshape(out_ref.shape[1:])
             return 0
 
         lax.fori_loop(0, groups, group, 0)
-
-    for g in range(groups):
-        result(g).wait()
     for ref, sem in ((coeff, fwd_sent), (coeff, bwd_sent)):
         away = ref.at[:, pl.ds(0, count - 1)]
         pltpu.make_async_copy(away, away, sem).wait()
-
-
-def hand_on(pieces, in_ref, out_ref, held, got, sent):
-    size = in_ref.shape[0] // pieces
-    parts = [pl.ds(i * size, size) for i in range(pieces)]
-    inward = [pltpu.make_async_copy(in_ref.at[p], held.at[p], got.at[i]) for i, p in enumerate(parts)]
-    outward = [pltpu.make_async_copy(held.at[p], out_ref.at[p], sent.at[i]) for i, p in enumerate(parts)]
-    for copy in inward:
-        copy.start()
-    for before, after in zip(inward, outward):
-        before.wait()
-        after.start()
-    for copy in outward:
-        copy.wait()
 
 
 def on_device_rows(spec_in, legendre, mode_slot, w_in, b_in, w_out, kernel):
@@ -382,9 +360,9 @@
     bf16, f32 = jnp.bfloat16, jnp.float32
     out = pl.pallas_call(
         functools.partial(rows_kernel, lats, chans, chunks, columns),
-        out_shape=jax.ShapeDtypeStruct((slots, width, 2, degrees), bf16),
+        out_shape=pltpu.VMEM((slots, width, 2, degrees), bf16),
         in_specs=[smem] + [hbm] * 2 + [vmem] * 4,
-        out_specs=hbm,
+        out_specs=vmem,
         scratch_shapes=[
             pltpu.VMEM((2, GROUP, span, degrees), f32),
             pltpu.VMEM((slots, width, 2, degrees), bf16),
@@ -404,29 +382,14 @@
             pltpu.VMEM((lats * depth, width), f32),
             pltpu.SemaphoreType.DMA((2,)),
             pltpu.SemaphoreType.DMA((groups,)),
-            pltpu.SemaphoreType.DMA((groups,)),
             pltpu.SemaphoreType.DMA,
             pltpu.SemaphoreType.DMA((chunks,)),
             pltpu.SemaphoreType.DMA,
             pltpu.SemaphoreType.DMA((chunks + groups - 1,)),
         ],
-        compiler_params=pltpu.CompilerParams(vmem_limit_bytes=61 * 1024 * 1024, has_side_effects=True, collective_id=0),
+        compiler_params=pltpu.CompilerParams(vmem_limit_bytes=52 * 1024 * 1024, has_side_effects=True, collective_id=0),
         name="rows",
     )(mode_slot, spec_in[:, 0], legendre, kernel.T, w_in, b_in[None, :], w_out)
-    pieces = next(n for n in (8, 6, 4, 3, 2, 1) if slots % n == 0)
-    out = pl.pallas_call(
-        functools.partial(hand_on, pieces),
-        out_shape=jax.ShapeDtypeStruct(out.shape, bf16),
-        in_specs=[hbm],
-        out_specs=hbm,
-        scratch_shapes=[
-            pltpu.VMEM(out.shape, bf16),
-            pltpu.SemaphoreType.DMA((pieces,)),
-            pltpu.SemaphoreType.DMA((pieces,)),
-        ],
-        compiler_params=pltpu.CompilerParams(vmem_limit_bytes=61 * 1024 * 1024),
-        name="hand_on",
-    )(out)
     return out[:, None]
 
 

time: 220 us -> 217 us (0.986)
  Pallas kernels: 219 us -> 214 us
    pallas_call x1 -> x0, Pallas kernels: 4.12 us -> none  [on_device_rows(): pl.pallas_call(functools.partial(hand_on, pieces), out_shape=jax.ShapeDty...]
where the time goes in v5:
time: 217 us; the launch traced here: 216 us
  Pallas kernels  214 us (99%)
  local copies, waits for them, and re-layouts  2.19 us (1%)
    pallas_call x1, Pallas kernels, on_device_rows(): pl.pallas_call(functools.partial(rows_kernel, lats, chans, chunks, column...  214 us

profile of v5, /device:TPU:11, one launch (start us, length us, event | category | flops | bytes accessed | tf_op | source)
XLA Modules:
  0.0 216.0 jit_solution(12414789572930290758)
XLA Ops:
  0.0 213.8 %rows.1 = bf16[24,128,2,384]{3,2,1,0:T(2,128)(2,1)S(1)} custom-call(s32[384]{0:T(512)} %mode_ref.1, bf16[24,128,2,384]{3,2,1,0:T(2,128)(2,1)} %bitcast.7, f32[24,384,384]{2,1,0:T(8,128)} %legendre_ref.1, f32[9,128]{1,0:T(8,128)} %bitcast.8, bf16[512,256]{1,0:T(8,128)(2,1)} %w_in_ref.1, f32[1,512]{1,0:T(1,128)} %bitcast.9, bf16[256,512]{1,0:T(8,128)(2,1)} %w_out_ref.1), custom_call_target="tpu_custom_call" | custom-call | tf_op jit(solution)/shard_map/rows/pallas_call | solution.py:361
  213.8 2.2 %copy.10 = bf16[24,1,128,2,384]{4,3,2,1,0:T(2,128)(2,1)} copy(bf16[24,1,128,2,384]{4,3,2,1,0:T(2,128)(2,1)S(1)} %bitcast.6) | data formatting | bytes 9437184

commit v6 on v5

--- a/solution.py
+++ b/solution.py
@@ -96,7 +96,7 @@
 
 def rows_kernel(lats, chans, chunks, columns, mode_ref, spec_ref, legendre_ref, taps_ref,
                 w_in_ref, b_in_ref, w_out_ref, out_ref,
-                raw, spec, table, stage, coeff, recv, send, got, mix, field, waves, waves_t, filters, perm, perm_t, marks,
+                raw, spec, table, stage, coeff, recv, send, got, mix, field, waves, waves_t, filters, perm, perm_t, marks, early,
                 raw_got, spec_got, fwd_sent, fwd_got, bwd_sent, bwd_got):
     span, degrees = raw.shape[2:]
     slots = table.shape[0]
@@ -297,6 +297,10 @@
         def group(g, _):
             part = pl.ds(pl.multiple_of(g * pair, pair), pair)
             if k == chunks - 1:
+                for i in range(GROUP if low else 0):
+                    s = g * GROUP + i
+                    early[i] = lax.dot_general(
+                        field[s, :low], table[s, :low], (((0,), (0,)), ((), ())), preferred_element_type=f32)
                 last = got.at[arrived, part, :]
                 pltpu.make_async_copy(last, last, bwd_got.at[k + g]).wait()
             own = pl.ds(pl.multiple_of(g * GROUP, GROUP), GROUP)
@@ -335,7 +339,9 @@
                 for i in range(GROUP):
                     s = g * GROUP + i
                     out = lax.dot_general(
-                        field[s], table[s], (((0,), (0,)), ((), ())), preferred_element_type=f32)
+                        field[s, low:], table[s, low:], (((0,), (0,)), ((), ())), preferred_element_type=f32)
+                    if low:
+                        out = out + early[i]
                     out_ref[s] = out.astype(bf16).reshape(out_ref.shape[1:])
             return 0
 
@@ -380,6 +386,7 @@
             pltpu.VMEM((2 * width, 2 * width), bf16),
             pltpu.VMEM((2 * width, 2 * width), bf16),
             pltpu.VMEM((lats * depth, width), f32),
+            pltpu.VMEM((GROUP, 2 * width, degrees), f32),
             pltpu.SemaphoreType.DMA((2,)),
             pltpu.SemaphoreType.DMA((groups,)),
             pltpu.SemaphoreType.DMA,
@@ -387,7 +394,7 @@
             pltpu.SemaphoreType.DMA,
             pltpu.SemaphoreType.DMA((chunks + groups - 1,)),
         ],
-        compiler_params=pltpu.CompilerParams(vmem_limit_bytes=52 * 1024 * 1024, has_side_effects=True, collective_id=0),
+        compiler_params=pltpu.CompilerParams(vmem_limit_bytes=54 * 1024 * 1024, has_side_effects=True, collective_id=0),
         name="rows",
     )(mode_slot, spec_in[:, 0], legendre, kernel.T, w_in, b_in[None, :], w_out)
     return out[:, None]

time: 217 us -> 216 us (level)
  no operation moved by 1% of the time
where the time goes in v6:
time: 216 us
  Pallas kernels  213 us (99%)
  local copies, waits for them, and re-layouts  2.19 us (1%)
    pallas_call x1, Pallas kernels, on_device_rows(): pl.pallas_call(functools.partial(rows_kernel, lats, chans, chunks, column...  213 us

profile of v6, /device:TPU:11, one launch (start us, length us, event | category | flops | bytes accessed | tf_op | source)
XLA Modules:
  0.0 215.5 jit_solution(5552096920004323655)
XLA Ops:
  0.0 213.3 %rows.1 = bf16[24,128,2,384]{3,2,1,0:T(2,128)(2,1)S(1)} custom-call(s32[384]{0:T(512)} %mode_ref.1, bf16[24,128,2,384]{3,2,1,0:T(2,128)(2,1)} %bitcast.7, f32[24,384,384]{2,1,0:T(8,128)} %legendre_ref.1, f32[9,128]{1,0:T(8,128)} %bitcast.8, bf16[512,256]{1,0:T(8,128)(2,1)} %w_in_ref.1, f32[1,512]{1,0:T(1,128)} %bitcast.9, bf16[256,512]{1,0:T(8,128)(2,1)} %w_out_ref.1), custom_call_target="tpu_custom_call" | custom-call | tf_op jit(solution)/shard_map/rows/pallas_call | solution.py:367
  213.3 2.2 %copy.10 = bf16[24,1,128,2,384]{4,3,2,1,0:T(2,128)(2,1)} copy(bf16[24,1,128,2,384]{4,3,2,1,0:T(2,128)(2,1)S(1)} %bitcast.6) | data formatting | bytes 9437184
